TPU v7x, 32 devices: a whole 2x2x4 slice. The times are simulated.
32 devices in a mesh: blk: 8 (over z, x), grp: 4 (over y, core).
Axes of the slice: x: 2, y: 2, z: 4, core: 2. Of those that a mesh axis runs over, the one named last changes fastest.
Arguments:
- query_rows: bfloat16 [4096, 128], P(('blk', 'grp')), may hold values from -36 to 36
- key_rows: bfloat16 [4096, 128], P(('blk', 'grp')), may hold values from -6 to 6
- value_rows: bfloat16 [4096, 128], P(('blk', 'grp')), may hold values from -6 to 6
- query_tangent: bfloat16 [4096, 128], P(('blk', 'grp')), may hold values from -6 to 6
- key_tangent: bfloat16 [4096, 128], P(('blk', 'grp')), may hold values from -6 to 6
- value_tangent: bfloat16 [4096, 128], P(('blk', 'grp')), may hold values from -6 to 6
Outputs:
- attended: float32 [4096, 128], P(('blk', 'grp'))
- tangent_out: float32 [4096, 128], P(('blk', 'grp'))
All inputs are finite; a program needn't handle non-finite values.
Results may differ from a plain program's by a relative error of at most 0.02.
Values may be sent and summed in bfloat16 or wider, within the bound.
No kernel may reach another device: no remote copies, remote signals or barrier semaphores. Data moves between devices by JAX's collectives and lax.ppermute only.
A program may use at most 128 MiB of HBM per device.

v0:
```python
import functools

import jax
import jax.numpy as jnp
from jax import lax
from jax.experimental import pallas as pl
from jax.experimental.pallas import tpu as pltpu
from jax.sharding import PartitionSpec as P


TAIL = 8
VMEM = pl.BlockSpec(memory_space=pltpu.VMEM)


def pack_kernel(k, dk, v, dv, q, dq, kv_out, q_out, sems):
    head = k.shape[1]
    places = [
        (k, kv_out, 0), (dk, kv_out, 1), (v, kv_out, 2), (dv, kv_out, 3),
        (dq, q_out, 0), (q, q_out, 1),
    ]
    copies = [
        pltpu.make_async_copy(src, out.at[:, at * head : (at + 1) * head], sems.at[i])
        for i, (src, out, at) in enumerate(places)
    ]
    for copy in copies:
        copy.start()
    for copy in copies:
        copy.wait()


def split3(x):
    hi = x.astype(jnp.bfloat16).astype(jnp.float32)
    mid = (x - hi).astype(jnp.bfloat16).astype(jnp.float32)
    return hi, mid, x - hi - mid


def panel_kernel(count, scale, q_ref, near_ref, far_ref, own_ref, stat_ref, *send_refs):
    rows, width = own_ref.shape
    head = width // 2
    nt = (((1,), (1,)), ((), ()))
    nn = (((1,), (0,)), ((), ()))
    f32 = jnp.float32
    lane = lax.broadcasted_iota(jnp.int32, (rows, head), 1)
    for block in range(count):
        q = q_ref[block * rows : (block + 1) * rows, :]
        primal_q = q[:, head:]
        scores = [
            lax.dot_general(primal_q, kv[:, :head], nt, preferred_element_type=f32)
            for kv in (near_ref, far_ref)
        ]
        slopes = [
            lax.dot_general(q, kv[:, :width], nt, preferred_element_type=f32)
            for kv in (near_ref, far_ref)
        ]
        top = functools.reduce(
            jnp.maximum, [jnp.max(s, axis=1, keepdims=True) for s in scores]
        )
        total = slope_total = both = slope_part = None
        for s, d, kv in zip(scores, slopes, (near_ref, far_ref)):
            probs = jnp.exp((s - top) * scale)
            weighted = probs * d
            a = jnp.sum(probs, axis=1, keepdims=True)
            b = jnp.sum(weighted, axis=1, keepdims=True)
            c = lax.dot_general(
                probs.astype(jnp.bfloat16), kv[:, width:], nn, preferred_element_type=f32
            )
            e = lax.dot_general(
                weighted.astype(jnp.bfloat16),
                kv[:, width : width + head],
                nn,
                preferred_element_type=f32,
            )
            if total is None:
                total, slope_total, both, slope_part = a, b, c, e
            else:
                total, slope_total = total + a, slope_total + b
                both, slope_part = both + c, slope_part + e
        inverse = 1.0 / total
        attended = both[:, :head] * inverse
        slope_mean = slope_total * (scale * inverse)
        tangent = (both[:, head:] + slope_part * scale) * inverse - slope_mean * attended
        lse = top * scale + jnp.log(total)
        if block == 0:
            own_ref[:, :head] = attended
            own_ref[:, head:] = tangent
            stat_ref[...] = jnp.where(lane == 0, lse, slope_mean)
        else:
            out = send_refs[block - 1]
            out[:rows, :head] = attended.astype(jnp.bfloat16)
            out[:rows, head:] = tangent.astype(jnp.bfloat16)
            pieces = split3(lse) + split3(slope_mean)
            tile = jnp.zeros((rows, head), f32)
            for at, piece in enumerate(pieces):
                tile = jnp.where(lane == at, piece, tile)
            out[rows:, :head] = tile.T[:TAIL, :].astype(jnp.bfloat16)
            out[rows:, head:] = jnp.zeros((TAIL, head), jnp.bfloat16)


def merge_kernel(own_ref, stat_ref, *refs):
    got_refs, (attended_ref, tangent_ref) = refs[:-2], refs[-2:]
    rows, head = attended_ref.shape
    f32 = jnp.float32
    parts = [(own_ref[:, :head], own_ref[:, head:], stat_ref[:, 0:1], stat_ref[:, 1:2])]
    for got in got_refs:
        cols = got[rows:, :head].astype(f32).T
        parts.append(
            (
                got[:rows, :head].astype(f32),
                got[:rows, head:].astype(f32),
                cols[:, 0:1] + cols[:, 1:2] + cols[:, 2:3],
                cols[:, 3:4] + cols[:, 4:5] + cols[:, 5:6],
            )
        )
    top = functools.reduce(jnp.maximum, [p[2] for p in parts])
    weights = [jnp.exp(p[2] - top) for p in parts]
    inverse = 1.0 / sum(weights)
    weights = [w * inverse for w in weights]
    mean = sum(w * p[3] for w, p in zip(weights, parts))
    attended_ref[...] = sum(w * p[0] for w, p in zip(weights, parts))
    tangent_ref[...] = sum(
        w * p[1] + (w * (p[3] - mean)) * p[0] for w, p in zip(weights, parts)
    )


def on_device(shape, query_rows, key_rows, value_rows, query_tangent, key_tangent, value_tangent):
    outer, inner, side, cores = shape
    plane = inner * side
    rows, head = query_rows.shape
    scale = head ** (-0.5)
    axes = ("blk", "grp")
    mix = lambda i, s, n: i ^ s if n & (n - 1) == 0 else (i + s) % n
    back = lambda i, s, n: i ^ s if n & (n - 1) == 0 else (i - s) % n

    def index(o, p, c):
        return (o * plane + p) * cores + c

    every = [(o, p, c) for o in range(outer) for p in range(plane) for c in range(cores)]
    over_plane = lambda s: [(index(o, p, c), index(o, mix(p, s, plane), c)) for o, p, c in every]
    over_core = [(index(o, p, c), index(o, p, (c + 1) % cores)) for o, p, c in every]
    over_outer = lambda s: [(index(o, p, c), index(mix(o, s, outer), p, c)) for o, p, c in every]
    outer_back = lambda s: [(index(o, p, c), index(back(o, s, outer), p, c)) for o, p, c in every]

    kv, q = pl.pallas_call(
        pack_kernel,
        out_shape=(
            jax.ShapeDtypeStruct((rows, 4 * head), key_rows.dtype),
            jax.ShapeDtypeStruct((rows, 2 * head), key_rows.dtype),
        ),
        in_specs=[pl.BlockSpec(memory_space=pltpu.HBM)] * 6,
        out_specs=(VMEM, VMEM),
        scratch_shapes=[pltpu.SemaphoreType.DMA((6,))],
        compiler_params=pltpu.CompilerParams(vmem_limit_bytes=8 * 2**20),
        name="pack",
    )(
        *(
            pltpu.with_memory_space_constraint(x, pltpu.HBM)
            for x in (key_rows, key_tangent, value_rows, value_tangent, query_rows, query_tangent)
        )
    )
    nears = [kv] + [lax.ppermute(kv, axes, over_plane(s)) for s in range(1, plane)]
    queries = [q] + [lax.ppermute(q, axes, over_outer(s)) for s in range(1, outer)]
    near = jnp.concatenate(nears, axis=0)
    far = lax.ppermute(near, axes, over_core)
    queries = jnp.concatenate(queries, axis=0)

    bf16, f32 = jnp.bfloat16, jnp.float32
    panel = pl.pallas_call(
        functools.partial(panel_kernel, outer, scale),
        out_shape=(
            jax.ShapeDtypeStruct((rows, 2 * head), f32),
            jax.ShapeDtypeStruct((rows, head), f32),
        )
        + tuple(jax.ShapeDtypeStruct((rows + TAIL, 2 * head), bf16) for _ in range(1, outer)),
        in_specs=[VMEM] * 3,
        out_specs=(VMEM,) * (1 + outer),
        compiler_params=pltpu.CompilerParams(vmem_limit_bytes=40 * 2**20),
        cost_estimate=pl.CostEstimate(
            flops=10 * queries.shape[0] * 2 * near.shape[0] * head,
            bytes_accessed=0,
            transcendentals=0,
        ),
        name="panel",
    )
    own, stat, *sends = panel(queries, near, far)
    gots = [
        lax.ppermute(block, axes, outer_back(s)) for s, block in zip(range(1, outer), sends)
    ]
    return pl.pallas_call(
        merge_kernel,
        out_shape=(jax.ShapeDtypeStruct((rows, head), f32),) * 2,
        in_specs=[VMEM] * (2 + len(gots)),
        out_specs=(VMEM, VMEM),
        compiler_params=pltpu.CompilerParams(vmem_limit_bytes=8 * 2**20),
        name="merge",
    )(own, stat, *gots)


def solution(mesh):
    blocks, group = mesh.shape["blk"], mesh.shape["grp"]
    cores = 2 if group % 2 == 0 else 1
    outer = group if blocks % group == 0 else 1
    shape = (outer, blocks // outer, group // cores, cores)
    placed = P(("blk", "grp"), None)

    def body(*args):
        return on_device(shape, *args)

    return jax.shard_map(
        body,
        mesh=mesh,
        in_specs=(placed,) * 6,
        out_specs=(placed, placed),
        check_vma=False,
    )
```

profile of v0, /device:TPU:0, one launch (start us, length us, event | category | flops | bytes accessed | tf_op | source)
XLA Modules:
  0.0 35.3 jit_solution(13154386591174892167)
XLA Ops:
  0.6 0.9 %pack.1 = (bf16[128,512]{1,0:T(8,128)(2,1)S(1)}, bf16[128,256]{1,0:T(8,128)(2,1)S(1)}) custom-call(bf16[128,128]{1,0:T(8,128)(2,1)} %k.1, bf16[128,128]{1,0:T(8,128)(2,1)} %dk.1, bf16[128,128]{1,0:T(8,128)(2,1)} %v.1, bf16[128,128]{1,0:T(8,128)(2,1)} %dv.1, bf16[128,128]{1,0:T(8,128)(2,1)} %q.1, bf16[128,128]{1,0:T(8,128)(2,1)} %dq.1), custom_call_target="tpu_custom_call" | custom-call | tf_op jit(solution)/shard_map/pack/pallas_call | solution.py:143
  1.5 3.1 %collective-permute-start.3 = (bf16[128,512]{1,0:T(8,128)(2,1)S(1)}, bf16[128,512]{1,0:T(8,128)(2,1)S(1)}, u32[]{:S(2)}, u32[]{:S(2)}) collective-permute-start(bf16[128,512]{1,0:T(8,128)(2,1)S(1)} %get-tuple-element.10), channel_id=1, source_target_pairs={{0,2},{1,3},{2,0},{3,1},{4,6},{5,7},{6,4},{7,5},{8,10},{9,11},{10,... | collective-permute-start | bytes 393224 | tf_op jit(solution)/shard_map/ppermute | solution.py:160
  4.6 1.4 %collective-permute-start.5 = (bf16[128,512]{1,0:T(8,128)(2,1)S(1)}, bf16[128,512]{1,0:T(8,128)(2,1)S(1)}, u32[]{:S(2)}, u32[]{:S(2)}) collective-permute-start(bf16[128,512]{1,0:T(8,128)(2,1)S(1)} %get-tuple-element.10), channel_id=1, source_target_pairs={{0,6},{1,7},{2,4},{3,5},{4,2},{5,3},{6,0},{7,1},{8,14},{9,15},{10,... | collective-permute-start | bytes 393224 | tf_op jit(solution)/shard_map/ppermute | solution.py:160
  6.0 0.1 collective-permute-start.4
  6.1 4.0 %collective-permute-done.3 = bf16[128,512]{1,0:T(8,128)(2,1)S(1)} collective-permute-done((bf16[128,512]{1,0:T(8,128)(2,1)S(1)}, bf16[128,512]{1,0:T(8,128)(2,1)S(1)}, u32[]{:S(2)}, u32[]{:S(2)}) %collective-permute-start.3) | collective-permute-done | bytes 131104 | tf_op jit(solution)/shard_map/ppermute | solution.py:160
  10.2 2.0 %collective-permute-done.4 = bf16[128,512]{1,0:T(8,128)(2,1)S(1)} collective-permute-done((bf16[128,512]{1,0:T(8,128)(2,1)S(1)}, bf16[128,512]{1,0:T(8,128)(2,1)S(1)}, u32[]{:S(2)}, u32[]{:S(2)}) %collective-permute-start.4) | collective-permute-done | bytes 131104 | tf_op jit(solution)/shard_map/ppermute | solution.py:160
  12.2 0.0 collective-permute-done.5
  12.2 0.1 collective-permute-start.6
  12.3 3.8 %collective-permute-start.2 = (bf16[128,256]{1,0:T(8,128)(2,1)S(1)}, bf16[128,256]{1,0:T(8,128)(2,1)S(1)}, u32[]{:S(2)}, u32[]{:S(2)}) collective-permute-start(bf16[128,256]{1,0:T(8,128)(2,1)S(1)} %get-tuple-element.9), channel_id=1, source_target_pairs={{0,24},{1,25},{2,26},{3,27},{4,28},{5,29},{6,30},{7,31},{8,16},{9,... | collective-permute-start | bytes 196616 | tf_op jit(solution)/shard_map/ppermute | solution.py:161
  16.1 0.0 collective-permute-start.1
  16.1 0.6 %collective-permute-start = (bf16[128,256]{1,0:T(8,128)(2,1)S(1)}, bf16[128,256]{1,0:T(8,128)(2,1)S(1)}, u32[]{:S(2)}, u32[]{:S(2)}) collective-permute-start(bf16[128,256]{1,0:T(8,128)(2,1)S(1)} %get-tuple-element.9), channel_id=1, source_target_pairs={{0,8},{1,9},{2,10},{3,11},{4,12},{5,13},{6,14},{7,15},{8,0},{9,1},... | collective-permute-start | bytes 196616 | tf_op jit(solution)/shard_map/ppermute | solution.py:161
  16.8 2.2 %collective-permute-done.2 = bf16[128,256]{1,0:T(8,128)(2,1)S(1)} collective-permute-done((bf16[128,256]{1,0:T(8,128)(2,1)S(1)}, bf16[128,256]{1,0:T(8,128)(2,1)S(1)}, u32[]{:S(2)}, u32[]{:S(2)}) %collective-permute-start.2) | collective-permute-done | bytes 65568 | tf_op jit(solution)/shard_map/ppermute | solution.py:161
  19.0 3.2 %collective-permute-done.1 = bf16[128,256]{1,0:T(8,128)(2,1)S(1)} collective-permute-done((bf16[128,256]{1,0:T(8,128)(2,1)S(1)}, bf16[128,256]{1,0:T(8,128)(2,1)S(1)}, u32[]{:S(2)}, u32[]{:S(2)}) %collective-permute-start.1) | collective-permute-done | bytes 65568 | tf_op jit(solution)/shard_map/ppermute | solution.py:161
  22.2 0.0 collective-permute-done
  22.2 0.0 collective-permute-done.6.far_ref
  22.2 2.3 %panel.1 = (f32[128,256]{1,0:T(8,128)S(1)}, f32[128,128]{1,0:T(8,128)S(1)}, bf16[136,256]{1,0:T(8,128)(2,1)S(1)}, bf16[136,256]{1,0:T(8,128)(2,1)S(1)}, bf16[136,256]{1,0:T(8,128)(2,1)S(1)}) custom-call(bf16[512,256]{1,0:T(8,128)(2,1)S(1)} %pad_maximum_fusion.q_ref, bf16[512,512]{1,0:T(8,128)(2,1)S(1)} %constant_dynamic-update-slice_fusion.near_ref, ...), custom_call_target="tpu_custom_call" | custom-call | flops 671088640 | tf_op jit(solution)/shard_map/panel/pallas_call | solution.py:184
  24.6 1.3 %collective-permute-start.7 = (bf16[136,256]{1,0:T(8,128)(2,1)S(1)}, bf16[136,256]{1,0:T(8,128)(2,1)S(1)}, u32[]{:S(2)}, u32[]{:S(2)}) collective-permute-start(bf16[136,256]{1,0:T(8,128)(2,1)S(1)} %get-tuple-element.13), channel_id=1, source_target_pairs={{0,8},{1,9},{2,10},{3,11},{4,12},{5,13},{6,14},{7,15},{8,0},{9,1},... | collective-permute-start | bytes 208904 | tf_op jit(solution)/shard_map/ppermute | solution.py:186
  25.8 1.8 %collective-permute-start.8 = (bf16[136,256]{1,0:T(8,128)(2,1)S(1)}, bf16[136,256]{1,0:T(8,128)(2,1)S(1)}, u32[]{:S(2)}, u32[]{:S(2)}) collective-permute-start(bf16[136,256]{1,0:T(8,128)(2,1)S(1)} %get-tuple-element.14), channel_id=1, source_target_pairs={{0,16},{1,17},{2,18},{3,19},{4,20},{5,21},{6,22},{7,23},{8,24},{9,... | collective-permute-start | bytes 208904 | tf_op jit(solution)/shard_map/ppermute | solution.py:186
  27.6 1.3 %collective-permute-start.9 = (bf16[136,256]{1,0:T(8,128)(2,1)S(1)}, bf16[136,256]{1,0:T(8,128)(2,1)S(1)}, u32[]{:S(2)}, u32[]{:S(2)}) collective-permute-start(bf16[136,256]{1,0:T(8,128)(2,1)S(1)} %get-tuple-element.15), channel_id=1, source_target_pairs={{0,24},{1,25},{2,26},{3,27},{4,28},{5,29},{6,30},{7,31},{8,16},{9,... | collective-permute-start | bytes 208904 | tf_op jit(solution)/shard_map/ppermute | solution.py:186
  29.0 0.5 %collective-permute-done.7.refs_0_ = bf16[136,256]{1,0:T(8,128)(2,1)S(1)} collective-permute-done((bf16[136,256]{1,0:T(8,128)(2,1)S(1)}, bf16[136,256]{1,0:T(8,128)(2,1)S(1)}, u32[]{:S(2)}, u32[]{:S(2)}) %collective-permute-start.7) | collective-permute-done | bytes 69664 | tf_op jit(solution)/shard_map/ppermute | solution.py:186
  29.5 3.6 %collective-permute-done.8.refs_1_ = bf16[136,256]{1,0:T(8,128)(2,1)S(1)} collective-permute-done((bf16[136,256]{1,0:T(8,128)(2,1)S(1)}, bf16[136,256]{1,0:T(8,128)(2,1)S(1)}, u32[]{:S(2)}, u32[]{:S(2)}) %collective-permute-start.8) | collective-permute-done | bytes 69664 | tf_op jit(solution)/shard_map/ppermute | solution.py:186
  33.1 0.8 %collective-permute-done.9.refs_2_ = bf16[136,256]{1,0:T(8,128)(2,1)S(1)} collective-permute-done((bf16[136,256]{1,0:T(8,128)(2,1)S(1)}, bf16[136,256]{1,0:T(8,128)(2,1)S(1)}, u32[]{:S(2)}, u32[]{:S(2)}) %collective-permute-start.9) | collective-permute-done | bytes 69664 | tf_op jit(solution)/shard_map/ppermute | solution.py:186
  33.9 1.5 %merge.1 = (f32[128,128]{1,0:T(8,128)}, f32[128,128]{1,0:T(8,128)}) custom-call(f32[128,256]{1,0:T(8,128)S(1)} %get-tuple-element.11.own_ref, f32[128,128]{1,0:T(8,128)S(1)} %get-tuple-element.12.stat_ref, bf16[136,256]{1,0:T(8,128)(2,1)S(1)} %collective-permute-done.7.refs_0_, bf16[136,256]{1,0:T(8,128)(2,1)S(1)} %collective-permute-done.8.refs_1_, ...), custom_call_target="tpu_custom_call" | custom-call | tf_op jit(solution)/shard_map/merge/pallas_call | solution.py:188
  (5 shorter events, 0.1 us)
Async XLA Ops:
  1.5 8.6 %collective-permute-start.3 = (bf16[128,512]{1,0:T(8,128)(2,1)S(1)}, bf16[128,512]{1,0:T(8,128)(2,1)S(1)}, u32[]{:S(2)}, u32[]{:S(2)}) collective-permute-start(bf16[128,512]{1,0:T(8,128)(2,1)S(1)} %get-tuple-element.10), channel_id=1, source_target_pairs={{0,2},{1,3},{2,0},{3,1},{4,6},{5,7},{6,4},{7,5},{8,10},{9,11},{10,... | collective-permute-start | bytes 393224 | tf_op jit(solution)/shard_map/ppermute | solution.py:160
  4.6 7.6 %collective-permute-start.5 = (bf16[128,512]{1,0:T(8,128)(2,1)S(1)}, bf16[128,512]{1,0:T(8,128)(2,1)S(1)}, u32[]{:S(2)}, u32[]{:S(2)}) collective-permute-start(bf16[128,512]{1,0:T(8,128)(2,1)S(1)} %get-tuple-element.10), channel_id=1, source_target_pairs={{0,6},{1,7},{2,4},{3,5},{4,2},{5,3},{6,0},{7,1},{8,14},{9,15},{10,... | collective-permute-start | bytes 393224 | tf_op jit(solution)/shard_map/ppermute | solution.py:160
  6.0 6.2 %collective-permute-start.4 = (bf16[128,512]{1,0:T(8,128)(2,1)S(1)}, bf16[128,512]{1,0:T(8,128)(2,1)S(1)}, u32[]{:S(2)}, u32[]{:S(2)}) collective-permute-start(bf16[128,512]{1,0:T(8,128)(2,1)S(1)} %get-tuple-element.10), channel_id=1, source_target_pairs={{0,4},{1,5},{2,6},{3,7},{4,0},{5,1},{6,2},{7,3},{8,12},{9,13},{10,... | collective-permute-start | bytes 393224 | tf_op jit(solution)/shard_map/ppermute | solution.py:160
  12.2 10.0 %collective-permute-start.6 = (bf16[512,512]{1,0:T(8,128)(2,1)S(1)}, bf16[512,512]{1,0:T(8,128)(2,1)S(1)}, u32[]{:S(2)}, u32[]{:S(2)}) collective-permute-start(bf16[512,512]{1,0:T(8,128)(2,1)S(1)} %constant_dynamic-update-slice_fusion.near_ref), channel_id=1, source_target_pairs={{0,1},{1,0},{2,3},{3,2},{4,5},{5,4},{6,7},{7,6},{8,9},{9,8},{10,11... | collective-permute-start | bytes 1572872 | tf_op jit(solution)/shard_map/ppermute | solution.py:163
  12.3 6.7 %collective-permute-start.2 = (bf16[128,256]{1,0:T(8,128)(2,1)S(1)}, bf16[128,256]{1,0:T(8,128)(2,1)S(1)}, u32[]{:S(2)}, u32[]{:S(2)}) collective-permute-start(bf16[128,256]{1,0:T(8,128)(2,1)S(1)} %get-tuple-element.9), channel_id=1, source_target_pairs={{0,24},{1,25},{2,26},{3,27},{4,28},{5,29},{6,30},{7,31},{8,16},{9,... | collective-permute-start | bytes 196616 | tf_op jit(solution)/shard_map/ppermute | solution.py:161
  16.1 6.1 %collective-permute-start.1 = (bf16[128,256]{1,0:T(8,128)(2,1)S(1)}, bf16[128,256]{1,0:T(8,128)(2,1)S(1)}, u32[]{:S(2)}, u32[]{:S(2)}) collective-permute-start(bf16[128,256]{1,0:T(8,128)(2,1)S(1)} %get-tuple-element.9), channel_id=1, source_target_pairs={{0,16},{1,17},{2,18},{3,19},{4,20},{5,21},{6,22},{7,23},{8,24},{9,... | collective-permute-start | bytes 196616 | tf_op jit(solution)/shard_map/ppermute | solution.py:161
  16.1 6.1 %collective-permute-start = (bf16[128,256]{1,0:T(8,128)(2,1)S(1)}, bf16[128,256]{1,0:T(8,128)(2,1)S(1)}, u32[]{:S(2)}, u32[]{:S(2)}) collective-permute-start(bf16[128,256]{1,0:T(8,128)(2,1)S(1)} %get-tuple-element.9), channel_id=1, source_target_pairs={{0,8},{1,9},{2,10},{3,11},{4,12},{5,13},{6,14},{7,15},{8,0},{9,1},... | collective-permute-start | bytes 196616 | tf_op jit(solution)/shard_map/ppermute | solution.py:161
  24.6 5.0 %collective-permute-start.7 = (bf16[136,256]{1,0:T(8,128)(2,1)S(1)}, bf16[136,256]{1,0:T(8,128)(2,1)S(1)}, u32[]{:S(2)}, u32[]{:S(2)}) collective-permute-start(bf16[136,256]{1,0:T(8,128)(2,1)S(1)} %get-tuple-element.13), channel_id=1, source_target_pairs={{0,8},{1,9},{2,10},{3,11},{4,12},{5,13},{6,14},{7,15},{8,0},{9,1},... | collective-permute-start | bytes 208904 | tf_op jit(solution)/shard_map/ppermute | solution.py:186
  25.8 7.3 %collective-permute-start.8 = (bf16[136,256]{1,0:T(8,128)(2,1)S(1)}, bf16[136,256]{1,0:T(8,128)(2,1)S(1)}, u32[]{:S(2)}, u32[]{:S(2)}) collective-permute-start(bf16[136,256]{1,0:T(8,128)(2,1)S(1)} %get-tuple-element.14), channel_id=1, source_target_pairs={{0,16},{1,17},{2,18},{3,19},{4,20},{5,21},{6,22},{7,23},{8,24},{9,... | collective-permute-start | bytes 208904 | tf_op jit(solution)/shard_map/ppermute | solution.py:186
  27.6 6.2 %collective-permute-start.9 = (bf16[136,256]{1,0:T(8,128)(2,1)S(1)}, bf16[136,256]{1,0:T(8,128)(2,1)S(1)}, u32[]{:S(2)}, u32[]{:S(2)}) collective-permute-start(bf16[136,256]{1,0:T(8,128)(2,1)S(1)} %get-tuple-element.15), channel_id=1, source_target_pairs={{0,24},{1,25},{2,26},{3,27},{4,28},{5,29},{6,30},{7,31},{8,16},{9,... | collective-permute-start | bytes 208904 | tf_op jit(solution)/shard_map/ppermute | solution.py:186
where the time goes:
time: 35.5 us; the launch traced here: 35.3 us
  waiting for transfers between devices  16.3 us (46%)
  starting transfers between devices  13.6 us (38%)
  Pallas kernels  4.68 us (13%)
  between operations  0.7 us (2%)
    ppermute x3, waiting for transfers between devices, on_device(): lax.ppermute(kv, axes, over_plane(s))  6.04 us
    ppermute x3, waiting for transfers between devices, on_device(): lax.ppermute(q, axes, over_outer(s))  5.41 us
    ppermute x3, waiting for transfers between devices, on_device(): lax.ppermute(block, axes, outer_back(s))  4.86 us
    ppermute x3, starting transfers between devices, on_device(): lax.ppermute(kv, axes, over_plane(s))  4.6 us
    ppermute x3, starting transfers between devices, on_device(): lax.ppermute(q, axes, over_outer(s))  4.46 us
    ppermute x3, starting transfers between devices, on_device(): lax.ppermute(block, axes, outer_back(s))  4.42 us
    pallas_call x1, Pallas kernels, on_device(): own, stat, *sends = panel(queries, near, far)  2.33 us
    pallas_call x1, Pallas kernels, on_device(): pl.pallas_call(merge_kernel, out_shape=(jax.ShapeDtypeStruct((rows, head)...  1.45 us
  transfers between devices with their start and end apart: 10, of which 7 were waited for; matrix products, arithmetic and copies ran while one was open for 0% of the time, Pallas kernels for 0%

commit v1 on v0

v1 whole, which is shorter than its diff:
```python
import functools
import math

import jax
import jax.numpy as jnp
from jax import lax
from jax.experimental import pallas as pl
from jax.experimental.pallas import tpu as pltpu
from jax.sharding import PartitionSpec as P


TAIL = 8
VMEM = pl.BlockSpec(memory_space=pltpu.VMEM)


def pack_kernel(k, dk, v, dv, q, dq, kv_out, q_out, sems):
    head = k.shape[1]
    places = [
        (k, kv_out, 0), (dk, kv_out, 1), (v, kv_out, 2), (dv, kv_out, 3),
        (dq, q_out, 0), (q, q_out, 1),
    ]
    copies = [
        pltpu.make_async_copy(src, out.at[:, at * head : (at + 1) * head], sems.at[i])
        for i, (src, out, at) in enumerate(places)
    ]
    for copy in copies:
        copy.start()
    for copy in copies:
        copy.wait()


def split3(x):
    hi = x.astype(jnp.bfloat16).astype(jnp.float32)
    mid = (x - hi).astype(jnp.bfloat16).astype(jnp.float32)
    return hi, mid, x - hi - mid


def panel_kernel(scale, keeps, count, *refs):
    q_refs, (near_ref, far_ref), outs = refs[:count], refs[count : count + 2], refs[count + 2 :]
    rows, width = q_refs[0].shape
    head = width // 2
    nt = (((1,), (1,)), ((), ()))
    nn = (((1,), (0,)), ((), ()))
    f32 = jnp.float32
    q = jnp.concatenate([ref[...] for ref in q_refs], axis=0)
    sides = (near_ref, far_ref)
    scores = [
        lax.dot_general(q[:, head:], kv[:, :head], nt, preferred_element_type=f32) for kv in sides
    ]
    slopes = [
        lax.dot_general(q, kv[:, :width], nt, preferred_element_type=f32) for kv in sides
    ]
    top = functools.reduce(jnp.maximum, [jnp.max(s, axis=1, keepdims=True) for s in scores])
    terms = []
    for s, d, kv in zip(scores, slopes, sides):
        probs = jnp.exp2((s - top) * (scale * math.log2(math.e)))
        weighted = probs * d
        terms.append(
            (
                jnp.sum(probs, axis=1, keepdims=True),
                jnp.sum(weighted, axis=1, keepdims=True),
                lax.dot_general(
                    probs.astype(jnp.bfloat16), kv[:, width:], nn, preferred_element_type=f32
                ),
                lax.dot_general(
                    weighted.astype(jnp.bfloat16),
                    kv[:, width : width + head],
                    nn,
                    preferred_element_type=f32,
                ),
            )
        )
    total, slope_total, both, slope_part = (x + y for x, y in zip(*terms))
    inverse = 1.0 / total
    attended = both[:, :head] * inverse
    slope_mean = slope_total * (scale * inverse)
    tangent = (both[:, head:] + slope_part * scale) * inverse - slope_mean * attended
    lse = top * scale + jnp.log(total)
    lane = lax.broadcasted_iota(jnp.int32, (rows, head), 1)
    row = lax.broadcasted_iota(jnp.int32, (TAIL, head), 0)
    for block in range(count):
        at = slice(block * rows, (block + 1) * rows)
        stats = jnp.where(lane % 2 == 0, lse[at], slope_mean[at]).T[:TAIL, :]
        if keeps and block == 0:
            outs[0][:, :head], outs[0][:, head:] = attended[at], tangent[at]
            outs[1][...] = stats
            continue
        out = outs[block + 1 if keeps else block]
        out[:rows, :head] = attended[at].astype(jnp.bfloat16)
        out[:rows, head:] = tangent[at].astype(jnp.bfloat16)
        high, middle, low = split3(stats)
        out[rows:, :head] = jnp.where(row < 2, high, low).astype(jnp.bfloat16)
        out[rows:, head:] = middle.astype(jnp.bfloat16)


def merge_kernel(own_ref, stat_ref, *refs):
    got_refs, (attended_ref, tangent_ref) = refs[:-2], refs[-2:]
    rows, head = attended_ref.shape
    f32 = jnp.float32
    parts = [(own_ref[:, :head], own_ref[:, head:])]
    lse, slope = [stat_ref[0:1, :]], [stat_ref[1:2, :]]
    for got in got_refs:
        ends, middle = got[rows:, :head].astype(f32), got[rows:, head:].astype(f32)
        lse.append(ends[0:1] + middle[0:1] + ends[2:3])
        slope.append(ends[1:2] + middle[1:2] + ends[3:4])
        parts.append((got[:rows, :head].astype(f32), got[:rows, head:].astype(f32)))
    top = functools.reduce(jnp.maximum, lse)
    weights = [jnp.exp(x - top) for x in lse]
    inverse = 1.0 / sum(weights)
    weights = [w * inverse for w in weights]
    mean = sum(w * s for w, s in zip(weights, slope))
    table = jnp.concatenate(weights + [w * (s - mean) for w, s in zip(weights, slope)], axis=0)
    columns = table.T
    n = len(parts)
    shares = [columns[:, i : i + 1] for i in range(n)]
    tilts = [columns[:, n + i : n + i + 1] for i in range(n)]
    attended_ref[...] = sum(w * p[0] for w, p in zip(shares, parts))
    tangent_ref[...] = sum(w * p[1] + t * p[0] for w, t, p in zip(shares, tilts, parts))


def on_device(shape, query_rows, key_rows, value_rows, query_tangent, key_tangent, value_tangent):
    outer, inner, side, cores = shape
    plane = inner * side
    rows, head = query_rows.shape
    scale = head ** (-0.5)
    axes = ("blk", "grp")
    mix = lambda i, s, n: i ^ s if n & (n - 1) == 0 else (i + s) % n
    back = lambda i, s, n: i ^ s if n & (n - 1) == 0 else (i - s) % n

    def index(o, p, c):
        return (o * plane + p) * cores + c

    every = [(o, p, c) for o in range(outer) for p in range(plane) for c in range(cores)]
    over_plane = lambda s: [(index(o, p, c), index(o, mix(p, s, plane), c)) for o, p, c in every]
    over_core = [(index(o, p, c), index(o, p, (c + 1) % cores)) for o, p, c in every]
    over_outer = lambda s: [(index(o, p, c), index(mix(o, s, outer), p, c)) for o, p, c in every]
    outer_back = lambda s: [(index(o, p, c), index(back(o, s, outer), p, c)) for o, p, c in every]

    kv, q = pl.pallas_call(
        pack_kernel,
        out_shape=(
            jax.ShapeDtypeStruct((rows, 4 * head), key_rows.dtype),
            jax.ShapeDtypeStruct((rows, 2 * head), key_rows.dtype),
        ),
        in_specs=[pl.BlockSpec(memory_space=pltpu.HBM)] * 6,
        out_specs=(VMEM, VMEM),
        scratch_shapes=[pltpu.SemaphoreType.DMA((6,))],
        compiler_params=pltpu.CompilerParams(vmem_limit_bytes=8 * 2**20),
        name="pack",
    )(
        *(
            pltpu.with_memory_space_constraint(x, pltpu.HBM)
            for x in (key_rows, key_tangent, value_rows, value_tangent, query_rows, query_tangent)
        )
    )

    def sent(x, pairs):
        return lax.ppermute(x, axes, pairs)

    nears = [kv] + [sent(kv, over_plane(s)) for s in range(1, plane)]
    queries = [q] + [sent(q, over_outer(s)) for s in range(1, outer)]
    near = jnp.concatenate(nears, axis=0)
    far = sent(near, over_core)

    f32 = jnp.float32
    part = jax.ShapeDtypeStruct((rows + TAIL, 2 * head), jnp.bfloat16)

    def panel(which):
        keeps = 0 in which
        outs = (part,) * (len(which) - keeps)
        if keeps:
            outs = (
                jax.ShapeDtypeStruct((rows, 2 * head), f32),
                jax.ShapeDtypeStruct((TAIL, head), f32),
            ) + outs
        return pl.pallas_call(
            functools.partial(panel_kernel, scale, keeps, len(which)),
            out_shape=outs,
            in_specs=[VMEM] * (len(which) + 2),
            out_specs=(VMEM,) * len(outs),
            compiler_params=pltpu.CompilerParams(vmem_limit_bytes=40 * 2**20),
            cost_estimate=pl.CostEstimate(
                flops=20 * len(which) * rows * near.shape[0] * head,
                bytes_accessed=0,
                transcendentals=0,
            ),
        )(*(queries[i] for i in which), near, far)

    sends = {s: panel((s,))[0] for s in range(2, outer)}
    own, stat, *rest = panel(tuple(range(min(2, outer))))
    sends.update(zip((1,), rest))
    gots = [sent(sends[s], outer_back(s)) for s in range(1, outer)]
    return pl.pallas_call(
        merge_kernel,
        out_shape=(jax.ShapeDtypeStruct((rows, head), f32),) * 2,
        in_specs=[VMEM] * (2 + len(gots)),
        out_specs=(VMEM, VMEM),
        compiler_params=pltpu.CompilerParams(vmem_limit_bytes=8 * 2**20),
        name="merge",
    )(own, stat, *gots)


def solution(mesh):
    blocks, group = mesh.shape["blk"], mesh.shape["grp"]
    cores = 2 if group % 2 == 0 else 1
    outer = group if blocks % group == 0 else 1
    shape = (outer, blocks // outer, group // cores, cores)
    placed = P(("blk", "grp"), None)

    def body(*args):
        return on_device(shape, *args)

    return jax.shard_map(
        body,
        mesh=mesh,
        in_specs=(placed,) * 6,
        out_specs=(placed, placed),
        check_vma=False,
    )
```

time: 35.5 us -> 31.7 us (0.89)
  waiting for transfers between devices: 16.3 us -> 12.3 us
  starting transfers between devices: 13.6 us -> 14.4 us
  Pallas kernels: 4.68 us -> 4.12 us
    ppermute x10, waiting for transfers between devices: 16.3 us -> 12.3 us  [sent(): return lax.ppermute(x, axes, pairs)]
    ppermute x10, starting transfers between devices: 13.6 us -> 14.4 us  [sent(): return lax.ppermute(x, axes, pairs)]
    pallas_call x1, Pallas kernels: 1.45 us -> 1 us  [on_device(): pl.pallas_call(merge_kernel, out_shape=(jax.ShapeDtypeStruct((rows, head)...]
    pallas_call x1 -> x3, Pallas kernels: 2.33 us -> 2.22 us  [panel(): pl.pallas_call(functools.partial(panel_kernel, scale, keeps, len(which)),...]
  transfers between devices with their start and end apart: 10 -> 10, of which waited for: 7 -> 6; matrix products, arithmetic and copies ran while one was open for 0% -> 0% of each run, Pallas kernels for 0% -> 7%
where the time goes in v1:
time: 31.7 us; the launch traced here: 31.5 us
  starting transfers between devices  14.4 us (45%)
  waiting for transfers between devices  12.3 us (39%)
  Pallas kernels  4.12 us (13%)
  between operations  0.68 us (2%)
    ppermute x10, starting transfers between devices, sent(): return lax.ppermute(x, axes, pairs)  14.4 us
    ppermute x10, waiting for transfers between devices, sent(): return lax.ppermute(x, axes, pairs)  12.3 us
    pallas_call x3, Pallas kernels, panel(): pl.pallas_call(functools.partial(panel_kernel, scale, keeps, len(which)),...  2.22 us
    pallas_call x1, Pallas kernels, on_device(): pl.pallas_call(merge_kernel, out_shape=(jax.ShapeDtypeStruct((rows, head)...  1 us
    pallas_call x1, Pallas kernels, on_device(): pl.pallas_call(pack_kernel, out_shape=(jax.ShapeDtypeStruct((rows, 4 * he...  0.89 us
  transfers between devices with their start and end apart: 10, of which 6 were waited for; matrix products, arithmetic and copies ran while one was open for 0% of the time, Pallas kernels for 7%

profile of v1, /device:TPU:0, one launch (start us, length us, event | category | flops | bytes accessed | tf_op | source)
XLA Modules:
  0.0 31.5 jit_solution(7050026937969706112)
XLA Ops:
  0.6 0.9 %pack.1 = (bf16[128,512]{1,0:T(8,128)(2,1)S(1)}, bf16[128,256]{1,0:T(8,128)(2,1)S(1)}) custom-call(bf16[128,128]{1,0:T(8,128)(2,1)} %k.1, bf16[128,128]{1,0:T(8,128)(2,1)} %dk.1, bf16[128,128]{1,0:T(8,128)(2,1)} %v.1, bf16[128,128]{1,0:T(8,128)(2,1)} %dv.1, bf16[128,128]{1,0:T(8,128)(2,1)} %q.1, bf16[128,128]{1,0:T(8,128)(2,1)} %dq.1), custom_call_target="tpu_custom_call" | custom-call | tf_op jit(solution)/shard_map/pack/pallas_call | solution.py:139
  1.5 3.1 %collective-permute-start.1 = (bf16[128,512]{1,0:T(8,128)(2,1)S(1)}, bf16[128,512]{1,0:T(8,128)(2,1)S(1)}, u32[]{:S(2)}, u32[]{:S(2)}) collective-permute-start(bf16[128,512]{1,0:T(8,128)(2,1)S(1)} %get-tuple-element.8), channel_id=1, source_target_pairs={{0,2},{1,3},{2,0},{3,1},{4,6},{5,7},{6,4},{7,5},{8,10},{9,11},{10,... | collective-permute-start | bytes 393224 | tf_op jit(solution)/shard_map/ppermute | solution.py:158
  4.6 1.5 %collective-permute-start.2 = (bf16[128,512]{1,0:T(8,128)(2,1)S(1)}, bf16[128,512]{1,0:T(8,128)(2,1)S(1)}, u32[]{:S(2)}, u32[]{:S(2)}) collective-permute-start(bf16[128,512]{1,0:T(8,128)(2,1)S(1)} %get-tuple-element.8), channel_id=1, source_target_pairs={{0,4},{1,5},{2,6},{3,7},{4,0},{5,1},{6,2},{7,3},{8,12},{9,13},{10,... | collective-permute-start | bytes 393224 | tf_op jit(solution)/shard_map/ppermute | solution.py:158
  6.1 0.0 collective-permute-start.3
  6.1 1.9 %collective-permute-done.1 = bf16[128,512]{1,0:T(8,128)(2,1)S(1)} collective-permute-done((bf16[128,512]{1,0:T(8,128)(2,1)S(1)}, bf16[128,512]{1,0:T(8,128)(2,1)S(1)}, u32[]{:S(2)}, u32[]{:S(2)}) %collective-permute-start.1) | collective-permute-done | bytes 131104 | tf_op jit(solution)/shard_map/ppermute | solution.py:158
  8.1 2.9 %collective-permute-done.2 = bf16[128,512]{1,0:T(8,128)(2,1)S(1)} collective-permute-done((bf16[128,512]{1,0:T(8,128)(2,1)S(1)}, bf16[128,512]{1,0:T(8,128)(2,1)S(1)}, u32[]{:S(2)}, u32[]{:S(2)}) %collective-permute-start.2) | collective-permute-done | bytes 131104 | tf_op jit(solution)/shard_map/ppermute | solution.py:158
  11.0 1.2 %collective-permute-done.3 = bf16[128,512]{1,0:T(8,128)(2,1)S(1)} collective-permute-done((bf16[128,512]{1,0:T(8,128)(2,1)S(1)}, bf16[128,512]{1,0:T(8,128)(2,1)S(1)}, u32[]{:S(2)}, u32[]{:S(2)}) %collective-permute-start.3) | collective-permute-done | bytes 131104 | tf_op jit(solution)/shard_map/ppermute | solution.py:158
  12.2 0.1 collective-permute-start.4
  12.2 1.8 %collective-permute-start = (bf16[128,256]{1,0:T(8,128)(2,1)S(1)}, bf16[128,256]{1,0:T(8,128)(2,1)S(1)}, u32[]{:S(2)}, u32[]{:S(2)}) collective-permute-start(bf16[128,256]{1,0:T(8,128)(2,1)S(1)} %get-tuple-element.7.refs_0_), channel_id=1, source_target_pairs={{0,8},{1,9},{2,10},{3,11},{4,12},{5,13},{6,14},{7,15},{8,0},{9,1},... | collective-permute-start | bytes 196616 | tf_op jit(solution)/shard_map/ppermute | solution.py:158
  14.0 2.6 %collective-permute-start.6 = (bf16[128,256]{1,0:T(8,128)(2,1)S(1)}, bf16[128,256]{1,0:T(8,128)(2,1)S(1)}, u32[]{:S(2)}, u32[]{:S(2)}) collective-permute-start(bf16[128,256]{1,0:T(8,128)(2,1)S(1)} %get-tuple-element.7.refs_0_), channel_id=1, source_target_pairs={{0,16},{1,17},{2,18},{3,19},{4,20},{5,21},{6,22},{7,23},{8,24},{9,... | collective-permute-start | bytes 196616 | tf_op jit(solution)/shard_map/ppermute | solution.py:158
  16.6 0.1 collective-permute-start.8
  16.7 0.0 collective-permute-done.refs_1_
  16.7 0.0 collective-permute-done.4.refs_3_.refs_2_
  16.7 0.9 %shard_map.77 = (f32[128,256]{1,0:T(8,128)S(1)}, f32[8,128]{1,0:T(8,128)S(1)}, bf16[136,256]{1,0:T(8,128)(2,1)S(1)}) custom-call(bf16[128,256]{1,0:T(8,128)(2,1)S(1)} %get-tuple-element.7.refs_0_, bf16[128,256]{1,0:T(8,128)(2,1)S(1)} %collective-permute-done.refs_1_, bf16[512,512]{1,0:T(8,128)(2,1)S(1)} %constant_dynamic-update-slice_fusion.refs_2_.refs_1_, ...), custom_call_target="tpu_custom_call" | custom-call | flops 335544320 | tf_op jit(solution)/shard_map/pallas_call | solution.py:176
  17.6 1.8 %collective-permute-start.5 = (bf16[136,256]{1,0:T(8,128)(2,1)S(1)}, bf16[136,256]{1,0:T(8,128)(2,1)S(1)}, u32[]{:S(2)}, u32[]{:S(2)}) collective-permute-start(bf16[136,256]{1,0:T(8,128)(2,1)S(1)} %get-tuple-element.11), channel_id=1, source_target_pairs={{0,8},{1,9},{2,10},{3,11},{4,12},{5,13},{6,14},{7,15},{8,0},{9,1},... | collective-permute-start | bytes 208904 | tf_op jit(solution)/shard_map/ppermute | solution.py:158
  19.4 2.3 %collective-permute-done.6.refs_0_ = bf16[128,256]{1,0:T(8,128)(2,1)S(1)} collective-permute-done((bf16[128,256]{1,0:T(8,128)(2,1)S(1)}, bf16[128,256]{1,0:T(8,128)(2,1)S(1)}, u32[]{:S(2)}, u32[]{:S(2)}) %collective-permute-start.6) | collective-permute-done | bytes 65568 | tf_op jit(solution)/shard_map/ppermute | solution.py:158
  21.8 0.7 %shard_map.78 = bf16[136,256]{1,0:T(8,128)(2,1)S(1)} custom-call(bf16[128,256]{1,0:T(8,128)(2,1)S(1)} %collective-permute-done.6.refs_0_, bf16[512,512]{1,0:T(8,128)(2,1)S(1)} %constant_dynamic-update-slice_fusion.refs_2_.refs_1_, bf16[512,512]{1,0:T(8,128)(2,1)S(1)} %collective-permute-done.4.refs_3_.refs_2_), custom_call_target="tpu_custom_call" | custom-call | flops 167772160 | tf_op jit(solution)/shard_map/pallas_call | solution.py:176
  22.4 1.2 %collective-permute-start.7 = (bf16[136,256]{1,0:T(8,128)(2,1)S(1)}, bf16[136,256]{1,0:T(8,128)(2,1)S(1)}, u32[]{:S(2)}, u32[]{:S(2)}) collective-permute-start(bf16[136,256]{1,0:T(8,128)(2,1)S(1)} %shard_map.78), channel_id=1, source_target_pairs={{0,16},{1,17},{2,18},{3,19},{4,20},{5,21},{6,22},{7,23},{8,24},{9,... | collective-permute-start | bytes 208904 | tf_op jit(solution)/shard_map/ppermute | solution.py:158
  23.6 0.0 collective-permute-done.8.refs_0_
  23.6 0.7 %shard_map.79 = bf16[136,256]{1,0:T(8,128)(2,1)S(1)} custom-call(bf16[128,256]{1,0:T(8,128)(2,1)S(1)} %collective-permute-done.8.refs_0_, bf16[512,512]{1,0:T(8,128)(2,1)S(1)} %constant_dynamic-update-slice_fusion.refs_2_.refs_1_, bf16[512,512]{1,0:T(8,128)(2,1)S(1)} %collective-permute-done.4.refs_3_.refs_2_), custom_call_target="tpu_custom_call" | custom-call | flops 167772160 | tf_op jit(solution)/shard_map/pallas_call | solution.py:176
  24.3 2.3 %collective-permute-start.9 = (bf16[136,256]{1,0:T(8,128)(2,1)S(1)}, bf16[136,256]{1,0:T(8,128)(2,1)S(1)}, u32[]{:S(2)}, u32[]{:S(2)}) collective-permute-start(bf16[136,256]{1,0:T(8,128)(2,1)S(1)} %shard_map.79), channel_id=1, source_target_pairs={{0,24},{1,25},{2,26},{3,27},{4,28},{5,29},{6,30},{7,31},{8,16},{9,... | collective-permute-start | bytes 208904 | tf_op jit(solution)/shard_map/ppermute | solution.py:158
  26.6 0.0 collective-permute-done.5.refs_0_
  26.6 2.6 %collective-permute-done.7.refs_1_ = bf16[136,256]{1,0:T(8,128)(2,1)S(1)} collective-permute-done((bf16[136,256]{1,0:T(8,128)(2,1)S(1)}, bf16[136,256]{1,0:T(8,128)(2,1)S(1)}, u32[]{:S(2)}, u32[]{:S(2)}) %collective-permute-start.7) | collective-permute-done | bytes 69664 | tf_op jit(solution)/shard_map/ppermute | solution.py:158
  29.1 1.3 %collective-permute-done.9.refs_2_ = bf16[136,256]{1,0:T(8,128)(2,1)S(1)} collective-permute-done((bf16[136,256]{1,0:T(8,128)(2,1)S(1)}, bf16[136,256]{1,0:T(8,128)(2,1)S(1)}, u32[]{:S(2)}, u32[]{:S(2)}) %collective-permute-start.9) | collective-permute-done | bytes 69664 | tf_op jit(solution)/shard_map/ppermute | solution.py:158
  30.5 1.0 %merge.1 = (f32[128,128]{1,0:T(8,128)}, f32[128,128]{1,0:T(8,128)}) custom-call(f32[128,256]{1,0:T(8,128)S(1)} %get-tuple-element.9.own_ref, f32[8,128]{1,0:T(8,128)S(1)} %get-tuple-element.10.stat_ref, bf16[136,256]{1,0:T(8,128)(2,1)S(1)} %collective-permute-done.5.refs_0_, bf16[136,256]{1,0:T(8,128)(2,1)S(1)} %collective-permute-done.7.refs_1_, ...), custom_call_target="tpu_custom_call" | custom-call | tf_op jit(solution)/shard_map/merge/pallas_call | solution.py:193
  (4 shorter events, 0.0 us)
Async XLA Ops:
  1.5 6.6 %collective-permute-start.1 = (bf16[128,512]{1,0:T(8,128)(2,1)S(1)}, bf16[128,512]{1,0:T(8,128)(2,1)S(1)}, u32[]{:S(2)}, u32[]{:S(2)}) collective-permute-start(bf16[128,512]{1,0:T(8,128)(2,1)S(1)} %get-tuple-element.8), channel_id=1, source_target_pairs={{0,2},{1,3},{2,0},{3,1},{4,6},{5,7},{6,4},{7,5},{8,10},{9,11},{10,... | collective-permute-start | bytes 393224 | tf_op jit(solution)/shard_map/ppermute | solution.py:158
  4.6 6.4 %collective-permute-start.2 = (bf16[128,512]{1,0:T(8,128)(2,1)S(1)}, bf16[128,512]{1,0:T(8,128)(2,1)S(1)}, u32[]{:S(2)}, u32[]{:S(2)}) collective-permute-start(bf16[128,512]{1,0:T(8,128)(2,1)S(1)} %get-tuple-element.8), channel_id=1, source_target_pairs={{0,4},{1,5},{2,6},{3,7},{4,0},{5,1},{6,2},{7,3},{8,12},{9,13},{10,... | collective-permute-start | bytes 393224 | tf_op jit(solution)/shard_map/ppermute | solution.py:158
  6.1 6.1 %collective-permute-start.3 = (bf16[128,512]{1,0:T(8,128)(2,1)S(1)}, bf16[128,512]{1,0:T(8,128)(2,1)S(1)}, u32[]{:S(2)}, u32[]{:S(2)}) collective-permute-start(bf16[128,512]{1,0:T(8,128)(2,1)S(1)} %get-tuple-element.8), channel_id=1, source_target_pairs={{0,6},{1,7},{2,4},{3,5},{4,2},{5,3},{6,0},{7,1},{8,14},{9,15},{10,... | collective-permute-start | bytes 393224 | tf_op jit(solution)/shard_map/ppermute | solution.py:158
  12.2 4.6 %collective-permute-start.4 = (bf16[512,512]{1,0:T(8,128)(2,1)S(1)}, bf16[512,512]{1,0:T(8,128)(2,1)S(1)}, u32[]{:S(2)}, u32[]{:S(2)}) collective-permute-start(bf16[512,512]{1,0:T(8,128)(2,1)S(1)} %constant_dynamic-update-slice_fusion.refs_2_.refs_1_), channel_id=1, source_target_pairs={{0,1},{1,0},{2,3},{3,2},{4,5},{5,4},{6,7},{7,6},{8,9},{9,8},{10,11... | collective-permute-start | bytes 1572872 | tf_op jit(solution)/shard_map/ppermute | solution.py:158
  12.2 4.5 %collective-permute-start = (bf16[128,256]{1,0:T(8,128)(2,1)S(1)}, bf16[128,256]{1,0:T(8,128)(2,1)S(1)}, u32[]{:S(2)}, u32[]{:S(2)}) collective-permute-start(bf16[128,256]{1,0:T(8,128)(2,1)S(1)} %get-tuple-element.7.refs_0_), channel_id=1, source_target_pairs={{0,8},{1,9},{2,10},{3,11},{4,12},{5,13},{6,14},{7,15},{8,0},{9,1},... | collective-permute-start | bytes 196616 | tf_op jit(solution)/shard_map/ppermute | solution.py:158
  14.0 7.7 %collective-permute-start.6 = (bf16[128,256]{1,0:T(8,128)(2,1)S(1)}, bf16[128,256]{1,0:T(8,128)(2,1)S(1)}, u32[]{:S(2)}, u32[]{:S(2)}) collective-permute-start(bf16[128,256]{1,0:T(8,128)(2,1)S(1)} %get-tuple-element.7.refs_0_), channel_id=1, source_target_pairs={{0,16},{1,17},{2,18},{3,19},{4,20},{5,21},{6,22},{7,23},{8,24},{9,... | collective-permute-start | bytes 196616 | tf_op jit(solution)/shard_map/ppermute | solution.py:158
  16.6 7.0 %collective-permute-start.8 = (bf16[128,256]{1,0:T(8,128)(2,1)S(1)}, bf16[128,256]{1,0:T(8,128)(2,1)S(1)}, u32[]{:S(2)}, u32[]{:S(2)}) collective-permute-start(bf16[128,256]{1,0:T(8,128)(2,1)S(1)} %get-tuple-element.7.refs_0_), channel_id=1, source_target_pairs={{0,24},{1,25},{2,26},{3,27},{4,28},{5,29},{6,30},{7,31},{8,16},{9,... | collective-permute-start | bytes 196616 | tf_op jit(solution)/shard_map/ppermute | solution.py:158
  17.6 9.0 %collective-permute-start.5 = (bf16[136,256]{1,0:T(8,128)(2,1)S(1)}, bf16[136,256]{1,0:T(8,128)(2,1)S(1)}, u32[]{:S(2)}, u32[]{:S(2)}) collective-permute-start(bf16[136,256]{1,0:T(8,128)(2,1)S(1)} %get-tuple-element.11), channel_id=1, source_target_pairs={{0,8},{1,9},{2,10},{3,11},{4,12},{5,13},{6,14},{7,15},{8,0},{9,1},... | collective-permute-start | bytes 208904 | tf_op jit(solution)/shard_map/ppermute | solution.py:158
  22.4 6.7 %collective-permute-start.7 = (bf16[136,256]{1,0:T(8,128)(2,1)S(1)}, bf16[136,256]{1,0:T(8,128)(2,1)S(1)}, u32[]{:S(2)}, u32[]{:S(2)}) collective-permute-start(bf16[136,256]{1,0:T(8,128)(2,1)S(1)} %shard_map.78), channel_id=1, source_target_pairs={{0,16},{1,17},{2,18},{3,19},{4,20},{5,21},{6,22},{7,23},{8,24},{9,... | collective-permute-start | bytes 208904 | tf_op jit(solution)/shard_map/ppermute | solution.py:158
  24.3 6.2 %collective-permute-start.9 = (bf16[136,256]{1,0:T(8,128)(2,1)S(1)}, bf16[136,256]{1,0:T(8,128)(2,1)S(1)}, u32[]{:S(2)}, u32[]{:S(2)}) collective-permute-start(bf16[136,256]{1,0:T(8,128)(2,1)S(1)} %shard_map.79), channel_id=1, source_target_pairs={{0,24},{1,25},{2,26},{3,27},{4,28},{5,29},{6,30},{7,31},{8,16},{9,... | collective-permute-start | bytes 208904 | tf_op jit(solution)/shard_map/ppermute | solution.py:158

commit v2 on v1

--- a/solution.py
+++ b/solution.py
@@ -35,30 +35,50 @@
     return hi, mid, x - hi - mid
 
 
-def panel_kernel(scale, keeps, count, *refs):
-    q_refs, (near_ref, far_ref), outs = refs[:count], refs[count : count + 2], refs[count + 2 :]
+def panel_kernel(scale, keeps, count, sides, resumes, ends, *refs):
+    q_refs, kv_refs, refs = refs[:count], refs[count : count + sides], refs[count + sides :]
+    state, outs = (refs[:2], refs[2:]) if resumes else ((), refs)
     rows, width = q_refs[0].shape
     head = width // 2
     nt = (((1,), (1,)), ((), ()))
     nn = (((1,), (0,)), ((), ()))
     f32 = jnp.float32
+    step = scale * math.log2(math.e)
     q = jnp.concatenate([ref[...] for ref in q_refs], axis=0)
-    sides = (near_ref, far_ref)
     scores = [
-        lax.dot_general(q[:, head:], kv[:, :head], nt, preferred_element_type=f32) for kv in sides
+        lax.dot_general(q[:, head:], kv[:, :head], nt, preferred_element_type=f32)
+        for kv in kv_refs
     ]
     slopes = [
-        lax.dot_general(q, kv[:, :width], nt, preferred_element_type=f32) for kv in sides
-    ]
-    top = functools.reduce(jnp.maximum, [jnp.max(s, axis=1, keepdims=True) for s in scores])
+        lax.dot_general(q, kv[:, :width], nt, preferred_element_type=f32) for kv in kv_refs
+    ]
+    tile = (q.shape[0], head)
+    over = lambda x, wide: jnp.concatenate([x] * (wide // head), axis=1)
+    tops = [
+        jnp.broadcast_to(jnp.max(s, axis=1, keepdims=True), tile) for s in scores
+    ]
+    if resumes:
+        sums_ref, lines_ref = state
+        tops.append(lines_ref[:, :head])
+    top = functools.reduce(jnp.maximum, tops)
     terms = []
-    for s, d, kv in zip(scores, slopes, sides):
-        probs = jnp.exp2((s - top) * (scale * math.log2(math.e)))
+    if resumes:
+        fade = jnp.exp2((tops[-1] - top) * step)
+        terms.append(
+            (
+                lines_ref[:, head:width] * fade,
+                lines_ref[:, width:] * fade,
+                sums_ref[:, :width] * over(fade, width),
+                sums_ref[:, width:] * fade,
+            )
+        )
+    for s, d, kv in zip(scores, slopes, kv_refs):
+        probs = jnp.exp2((s - over(top, s.shape[1])) * step)
         weighted = probs * d
         terms.append(
             (
-                jnp.sum(probs, axis=1, keepdims=True),
-                jnp.sum(weighted, axis=1, keepdims=True),
+                jnp.broadcast_to(jnp.sum(probs, axis=1, keepdims=True), tile),
+                jnp.broadcast_to(jnp.sum(weighted, axis=1, keepdims=True), tile),
                 lax.dot_general(
                     probs.astype(jnp.bfloat16), kv[:, width:], nn, preferred_element_type=f32
                 ),
@@ -70,7 +90,12 @@
                 ),
             )
         )
-    total, slope_total, both, slope_part = (x + y for x, y in zip(*terms))
+    total, slope_total, both, slope_part = (functools.reduce(jnp.add, x) for x in zip(*terms))
+    if not ends:
+        sums_ref, lines_ref = outs
+        sums_ref[:, :width], sums_ref[:, width:] = both, slope_part
+        lines_ref[...] = jnp.concatenate([top, total, slope_total], axis=1)
+        return
     inverse = 1.0 / total
     attended = both[:, :head] * inverse
     slope_mean = slope_total * (scale * inverse)
@@ -125,7 +150,6 @@
     scale = head ** (-0.5)
     axes = ("blk", "grp")
     mix = lambda i, s, n: i ^ s if n & (n - 1) == 0 else (i + s) % n
-    back = lambda i, s, n: i ^ s if n & (n - 1) == 0 else (i - s) % n
 
     def index(o, p, c):
         return (o * plane + p) * cores + c
@@ -133,8 +157,8 @@
     every = [(o, p, c) for o in range(outer) for p in range(plane) for c in range(cores)]
     over_plane = lambda s: [(index(o, p, c), index(o, mix(p, s, plane), c)) for o, p, c in every]
     over_core = [(index(o, p, c), index(o, p, (c + 1) % cores)) for o, p, c in every]
-    over_outer = lambda s: [(index(o, p, c), index(mix(o, s, outer), p, c)) for o, p, c in every]
-    outer_back = lambda s: [(index(o, p, c), index(back(o, s, outer), p, c)) for o, p, c in every]
+    over_outer = lambda s: [(index(o, p, c), index((o + s) % outer, p, c)) for o, p, c in every]
+    outer_back = lambda s: over_outer(outer - s)
 
     kv, q = pl.pallas_call(
         pack_kernel,
@@ -159,36 +183,46 @@
 
     nears = [kv] + [sent(kv, over_plane(s)) for s in range(1, plane)]
     queries = [q] + [sent(q, over_outer(s)) for s in range(1, outer)]
-    near = jnp.concatenate(nears, axis=0)
-    far = sent(near, over_core)
+    first = jnp.concatenate(nears[:-1], axis=0)
+    early = (first, sent(first, over_core))
+    late = (nears[-1], sent(nears[-1], over_core))
 
     f32 = jnp.float32
     part = jax.ShapeDtypeStruct((rows + TAIL, 2 * head), jnp.bfloat16)
 
-    def panel(which):
-        keeps = 0 in which
-        outs = (part,) * (len(which) - keeps)
-        if keeps:
+    def panel(which, sides, resumes=(), ends=True):
+        keeps = ends and 0 in which
+        n = len(which)
+        if not ends:
+            outs = (
+                jax.ShapeDtypeStruct((n * rows, 3 * head), f32),
+                jax.ShapeDtypeStruct((n * rows, 3 * head), f32),
+            )
+        elif keeps:
             outs = (
                 jax.ShapeDtypeStruct((rows, 2 * head), f32),
                 jax.ShapeDtypeStruct((TAIL, head), f32),
-            ) + outs
+            ) + (part,) * (n - 1)
+        else:
+            outs = (part,) * n
+        keys = sum(kv.shape[0] for kv in sides)
         return pl.pallas_call(
-            functools.partial(panel_kernel, scale, keeps, len(which)),
+            functools.partial(
+                panel_kernel, scale, keeps, n, len(sides), bool(resumes), ends
+            ),
             out_shape=outs,
-            in_specs=[VMEM] * (len(which) + 2),
+            in_specs=[VMEM] * (n + len(sides) + len(resumes)),
             out_specs=(VMEM,) * len(outs),
             compiler_params=pltpu.CompilerParams(vmem_limit_bytes=40 * 2**20),
             cost_estimate=pl.CostEstimate(
-                flops=20 * len(which) * rows * near.shape[0] * head,
-                bytes_accessed=0,
-                transcendentals=0,
+                flops=20 * n * rows * keys * head, bytes_accessed=0, transcendentals=0
             ),
-        )(*(queries[i] for i in which), near, far)
-
-    sends = {s: panel((s,))[0] for s in range(2, outer)}
-    own, stat, *rest = panel(tuple(range(min(2, outer))))
-    sends.update(zip((1,), rest))
+        )(*(queries[i] for i in which), *sides, *resumes)
+
+    remote = tuple(range(2, outer))
+    state = panel(remote, early, ends=False)
+    sends = dict(zip(remote, panel(remote, late, state)))
+    own, stat, sends[1] = panel((0, 1), early + late)
     gots = [sent(sends[s], outer_back(s)) for s in range(1, outer)]
     return pl.pallas_call(
         merge_kernel,

time: 31.7 us -> 38.5 us (1.21)
  waiting for transfers between devices: 12.3 us -> 18.5 us
  starting transfers between devices: 14.4 us -> 14.8 us
    ppermute x10 -> x11, waiting for transfers between devices: 12.3 us -> 18.5 us  [sent(): return lax.ppermute(x, axes, pairs)]
    ppermute x10 -> x11, starting transfers between devices: 14.4 us -> 14.8 us  [sent(): return lax.ppermute(x, axes, pairs)]
  transfers between devices with their start and end apart: 10 -> 11, of which waited for: 6 -> 7; matrix products, arithmetic and copies ran while one was open for 0% -> 0% of each run, Pallas kernels for 7% -> 6%
where the time goes in v2:
time: 38.5 us; the launch traced here: 38.3 us
  waiting for transfers between devices  18.5 us (48%)
  starting transfers between devices  14.8 us (38%)
  Pallas kernels  4.21 us (11%)
  between operations  0.69 us (2%)
    ppermute x11, waiting for transfers between devices, sent(): return lax.ppermute(x, axes, pairs)  18.5 us
    ppermute x11, starting transfers between devices, sent(): return lax.ppermute(x, axes, pairs)  14.8 us
    pallas_call x3, Pallas kernels, panel(): pl.pallas_call(functools.partial(panel_kernel, scale, keeps, n, len(sides...  2.32 us
    pallas_call x1, Pallas kernels, on_device(): pl.pallas_call(merge_kernel, out_shape=(jax.ShapeDtypeStruct((rows, head)...  1 us
    pallas_call x1, Pallas kernels, on_device(): pl.pallas_call(pack_kernel, out_shape=(jax.ShapeDtypeStruct((rows, 4 * he...  0.89 us
  transfers between devices with their start and end apart: 11, of which 7 were waited for; matrix products, arithmetic and copies ran while one was open for 0% of the time, Pallas kernels for 6%

profile of v2, /device:TPU:0, one launch (start us, length us, event | category | flops | bytes accessed | tf_op | source)
XLA Modules:
  0.0 38.3 jit_solution(8111876778266755490)
XLA Ops:
  0.6 0.9 %pack.1 = (bf16[128,512]{1,0:T(8,128)(2,1)S(1)}, bf16[128,256]{1,0:T(8,128)(2,1)S(1)}) custom-call(bf16[128,128]{1,0:T(8,128)(2,1)} %k.1, bf16[128,128]{1,0:T(8,128)(2,1)} %dk.1, bf16[128,128]{1,0:T(8,128)(2,1)} %v.1, bf16[128,128]{1,0:T(8,128)(2,1)} %dv.1, bf16[128,128]{1,0:T(8,128)(2,1)} %q.1, bf16[128,128]{1,0:T(8,128)(2,1)} %dq.1), custom_call_target="tpu_custom_call" | custom-call | tf_op jit(solution)/shard_map/pack/pallas_call | solution.py:163
  1.5 3.1 %collective-permute-start.1 = (bf16[128,512]{1,0:T(8,128)(2,1)S(1)}, bf16[128,512]{1,0:T(8,128)(2,1)S(1)}, u32[]{:S(2)}, u32[]{:S(2)}) collective-permute-start(bf16[128,512]{1,0:T(8,128)(2,1)S(1)} %get-tuple-element.12), channel_id=1, source_target_pairs={{0,2},{1,3},{2,0},{3,1},{4,6},{5,7},{6,4},{7,5},{8,10},{9,11},{10,... | collective-permute-start | bytes 393224 | tf_op jit(solution)/shard_map/ppermute | solution.py:182
  4.6 1.5 %collective-permute-start.2 = (bf16[128,512]{1,0:T(8,128)(2,1)S(1)}, bf16[128,512]{1,0:T(8,128)(2,1)S(1)}, u32[]{:S(2)}, u32[]{:S(2)}) collective-permute-start(bf16[128,512]{1,0:T(8,128)(2,1)S(1)} %get-tuple-element.12), channel_id=1, source_target_pairs={{0,4},{1,5},{2,6},{3,7},{4,0},{5,1},{6,2},{7,3},{8,12},{9,13},{10,... | collective-permute-start | bytes 393224 | tf_op jit(solution)/shard_map/ppermute | solution.py:182
  6.1 2.0 %collective-permute-done.1 = bf16[128,512]{1,0:T(8,128)(2,1)S(1)} collective-permute-done((bf16[128,512]{1,0:T(8,128)(2,1)S(1)}, bf16[128,512]{1,0:T(8,128)(2,1)S(1)}, u32[]{:S(2)}, u32[]{:S(2)}) %collective-permute-start.1) | collective-permute-done | bytes 131104 | tf_op jit(solution)/shard_map/ppermute | solution.py:182
  8.1 1.5 %collective-permute-done.2 = bf16[128,512]{1,0:T(8,128)(2,1)S(1)} collective-permute-done((bf16[128,512]{1,0:T(8,128)(2,1)S(1)}, bf16[128,512]{1,0:T(8,128)(2,1)S(1)}, u32[]{:S(2)}, u32[]{:S(2)}) %collective-permute-start.2) | collective-permute-done | bytes 131104 | tf_op jit(solution)/shard_map/ppermute | solution.py:182
  9.6 0.1 collective-permute-start.3
  9.7 1.5 %collective-permute-start.4 = (bf16[128,512]{1,0:T(8,128)(2,1)S(1)}, bf16[128,512]{1,0:T(8,128)(2,1)S(1)}, u32[]{:S(2)}, u32[]{:S(2)}) collective-permute-start(bf16[128,512]{1,0:T(8,128)(2,1)S(1)} %get-tuple-element.12), channel_id=1, source_target_pairs={{0,6},{1,7},{2,4},{3,5},{4,2},{5,3},{6,0},{7,1},{8,14},{9,15},{10,... | collective-permute-start | bytes 393224 | tf_op jit(solution)/shard_map/ppermute | solution.py:182
  11.2 5.3 %collective-permute-done.4.refs_4_.refs_2_ = bf16[128,512]{1,0:T(8,128)(2,1)S(1)} collective-permute-done((bf16[128,512]{1,0:T(8,128)(2,1)S(1)}, bf16[128,512]{1,0:T(8,128)(2,1)S(1)}, u32[]{:S(2)}, u32[]{:S(2)}) %collective-permute-start.4) | collective-permute-done | bytes 131104 | tf_op jit(solution)/shard_map/ppermute | solution.py:182
  16.5 0.0 collective-permute-start.5
  16.5 3.6 %collective-permute-start.8 = (bf16[128,256]{1,0:T(8,128)(2,1)S(1)}, bf16[128,256]{1,0:T(8,128)(2,1)S(1)}, u32[]{:S(2)}, u32[]{:S(2)}) collective-permute-start(bf16[128,256]{1,0:T(8,128)(2,1)S(1)} %get-tuple-element.11.refs_0_), channel_id=1, source_target_pairs={{0,24},{1,25},{2,26},{3,27},{4,28},{5,29},{6,30},{7,31},{8,0},{9,1... | collective-permute-start | bytes 196616 | tf_op jit(solution)/shard_map/ppermute | solution.py:182
  20.1 0.0 collective-permute-start.7
  20.1 1.0 %collective-permute-start = (bf16[128,256]{1,0:T(8,128)(2,1)S(1)}, bf16[128,256]{1,0:T(8,128)(2,1)S(1)}, u32[]{:S(2)}, u32[]{:S(2)}) collective-permute-start(bf16[128,256]{1,0:T(8,128)(2,1)S(1)} %get-tuple-element.11.refs_0_), channel_id=1, source_target_pairs={{0,8},{1,9},{2,10},{3,11},{4,12},{5,13},{6,14},{7,15},{8,16},{9,17... | collective-permute-start | bytes 196616 | tf_op jit(solution)/shard_map/ppermute | solution.py:182
  21.1 1.5 %collective-permute-done.8.refs_1_ = bf16[128,256]{1,0:T(8,128)(2,1)S(1)} collective-permute-done((bf16[128,256]{1,0:T(8,128)(2,1)S(1)}, bf16[128,256]{1,0:T(8,128)(2,1)S(1)}, u32[]{:S(2)}, u32[]{:S(2)}) %collective-permute-start.8) | collective-permute-done | bytes 65568 | tf_op jit(solution)/shard_map/ppermute | solution.py:182
  22.6 4.6 %collective-permute-done.7.refs_0_ = bf16[128,256]{1,0:T(8,128)(2,1)S(1)} collective-permute-done((bf16[128,256]{1,0:T(8,128)(2,1)S(1)}, bf16[128,256]{1,0:T(8,128)(2,1)S(1)}, u32[]{:S(2)}, u32[]{:S(2)}) %collective-permute-start.7) | collective-permute-done | bytes 65568 | tf_op jit(solution)/shard_map/ppermute | solution.py:182
  27.2 0.0 collective-permute-done.3.refs_3_
  27.2 0.8 %shard_map.78 = (f32[256,384]{1,0:T(8,128)S(1)}, f32[256,384]{1,0:T(8,128)S(1)}) custom-call(bf16[128,256]{1,0:T(8,128)(2,1)S(1)} %collective-permute-done.7.refs_0_, bf16[128,256]{1,0:T(8,128)(2,1)S(1)} %collective-permute-done.8.refs_1_, bf16[384,512]{1,0:T(8,128)(2,1)S(1)} %constant_dynamic-update-slice_fusion.refs_2_, ...), custom_call_target="tpu_custom_call" | custom-call | flops 503316480 | tf_op jit(solution)/shard_map/pallas_call | solution.py:209
  28.0 0.0 collective-permute-done.5.refs_5_.refs_3_
  28.0 0.6 %shard_map.79 = (bf16[136,256]{1,0:T(8,128)(2,1)S(1)}, bf16[136,256]{1,0:T(8,128)(2,1)S(1)}) custom-call(bf16[128,256]{1,0:T(8,128)(2,1)S(1)} %collective-permute-done.7.refs_0_, bf16[128,256]{1,0:T(8,128)(2,1)S(1)} %collective-permute-done.8.refs_1_, bf16[128,512]{1,0:T(8,128)(2,1)S(1)} %collective-permute-done.4.refs_4_.refs_2_, ...), custom_call_target="tpu_custom_call" | custom-call | flops 167772160 | tf_op jit(solution)/shard_map/pallas_call | solution.py:209
  28.6 0.2 collective-permute-start.9
  28.8 2.3 %collective-permute-start.10 = (bf16[136,256]{1,0:T(8,128)(2,1)S(1)}, bf16[136,256]{1,0:T(8,128)(2,1)S(1)}, u32[]{:S(2)}, u32[]{:S(2)}) collective-permute-start(bf16[136,256]{1,0:T(8,128)(2,1)S(1)} %get-tuple-element.19), channel_id=1, source_target_pairs={{0,8},{1,9},{2,10},{3,11},{4,12},{5,13},{6,14},{7,15},{8,16},{9,17... | collective-permute-start | bytes 208904 | tf_op jit(solution)/shard_map/ppermute | solution.py:182
  31.1 0.0 collective-permute-done.refs_1_
  31.1 0.9 %shard_map.77 = (f32[128,256]{1,0:T(8,128)S(1)}, f32[8,128]{1,0:T(8,128)S(1)}, bf16[136,256]{1,0:T(8,128)(2,1)S(1)}) custom-call(bf16[128,256]{1,0:T(8,128)(2,1)S(1)} %get-tuple-element.11.refs_0_, bf16[128,256]{1,0:T(8,128)(2,1)S(1)} %collective-permute-done.refs_1_, bf16[384,512]{1,0:T(8,128)(2,1)S(1)} %constant_dynamic-update-slice_fusion.refs_2_, ...), custom_call_target="tpu_custom_call" | custom-call | flops 671088640 | tf_op jit(solution)/shard_map/pallas_call | solution.py:209
  32.0 1.6 %collective-permute-start.6 = (bf16[136,256]{1,0:T(8,128)(2,1)S(1)}, bf16[136,256]{1,0:T(8,128)(2,1)S(1)}, u32[]{:S(2)}, u32[]{:S(2)}) collective-permute-start(bf16[136,256]{1,0:T(8,128)(2,1)S(1)} %get-tuple-element.15), channel_id=1, source_target_pairs={{0,24},{1,25},{2,26},{3,27},{4,28},{5,29},{6,30},{7,31},{8,0},{9,1... | collective-permute-start | bytes 208904 | tf_op jit(solution)/shard_map/ppermute | solution.py:182
  33.7 2.5 %collective-permute-done.9.refs_1_ = bf16[136,256]{1,0:T(8,128)(2,1)S(1)} collective-permute-done((bf16[136,256]{1,0:T(8,128)(2,1)S(1)}, bf16[136,256]{1,0:T(8,128)(2,1)S(1)}, u32[]{:S(2)}, u32[]{:S(2)}) %collective-permute-start.9) | collective-permute-done | bytes 69664 | tf_op jit(solution)/shard_map/ppermute | solution.py:182
  36.1 0.0 collective-permute-done.10.refs_2_
  36.1 1.2 %collective-permute-done.6.refs_0_ = bf16[136,256]{1,0:T(8,128)(2,1)S(1)} collective-permute-done((bf16[136,256]{1,0:T(8,128)(2,1)S(1)}, bf16[136,256]{1,0:T(8,128)(2,1)S(1)}, u32[]{:S(2)}, u32[]{:S(2)}) %collective-permute-start.6) | collective-permute-done | bytes 69664 | tf_op jit(solution)/shard_map/ppermute | solution.py:182
  37.3 1.0 %merge.1 = (f32[128,128]{1,0:T(8,128)}, f32[128,128]{1,0:T(8,128)}) custom-call(f32[128,256]{1,0:T(8,128)S(1)} %get-tuple-element.13.own_ref, f32[8,128]{1,0:T(8,128)S(1)} %get-tuple-element.14.stat_ref, bf16[136,256]{1,0:T(8,128)(2,1)S(1)} %collective-permute-done.6.refs_0_, bf16[136,256]{1,0:T(8,128)(2,1)S(1)} %collective-permute-done.9.refs_1_, ...), custom_call_target="tpu_custom_call" | custom-call | tf_op jit(solution)/shard_map/merge/pallas_call | solution.py:227
  (3 shorter events, 0.0 us)
Async XLA Ops:
  1.5 6.6 %collective-permute-start.1 = (bf16[128,512]{1,0:T(8,128)(2,1)S(1)}, bf16[128,512]{1,0:T(8,128)(2,1)S(1)}, u32[]{:S(2)}, u32[]{:S(2)}) collective-permute-start(bf16[128,512]{1,0:T(8,128)(2,1)S(1)} %get-tuple-element.12), channel_id=1, source_target_pairs={{0,2},{1,3},{2,0},{3,1},{4,6},{5,7},{6,4},{7,5},{8,10},{9,11},{10,... | collective-permute-start | bytes 393224 | tf_op jit(solution)/shard_map/ppermute | solution.py:182
  4.6 5.0 %collective-permute-start.2 = (bf16[128,512]{1,0:T(8,128)(2,1)S(1)}, bf16[128,512]{1,0:T(8,128)(2,1)S(1)}, u32[]{:S(2)}, u32[]{:S(2)}) collective-permute-start(bf16[128,512]{1,0:T(8,128)(2,1)S(1)} %get-tuple-element.12), channel_id=1, source_target_pairs={{0,4},{1,5},{2,6},{3,7},{4,0},{5,1},{6,2},{7,3},{8,12},{9,13},{10,... | collective-permute-start | bytes 393224 | tf_op jit(solution)/shard_map/ppermute | solution.py:182
  9.6 17.6 %collective-permute-start.3 = (bf16[384,512]{1,0:T(8,128)(2,1)S(1)}, bf16[384,512]{1,0:T(8,128)(2,1)S(1)}, u32[]{:S(2)}, u32[]{:S(2)}) collective-permute-start(bf16[384,512]{1,0:T(8,128)(2,1)S(1)} %constant_dynamic-update-slice_fusion.refs_2_), channel_id=1, source_target_pairs={{0,1},{1,0},{2,3},{3,2},{4,5},{5,4},{6,7},{7,6},{8,9},{9,8},{10,11... | collective-permute-start | bytes 1179656 | tf_op jit(solution)/shard_map/ppermute | solution.py:182
  9.7 6.8 %collective-permute-start.4 = (bf16[128,512]{1,0:T(8,128)(2,1)S(1)}, bf16[128,512]{1,0:T(8,128)(2,1)S(1)}, u32[]{:S(2)}, u32[]{:S(2)}) collective-permute-start(bf16[128,512]{1,0:T(8,128)(2,1)S(1)} %get-tuple-element.12), channel_id=1, source_target_pairs={{0,6},{1,7},{2,4},{3,5},{4,2},{5,3},{6,0},{7,1},{8,14},{9,15},{10,... | collective-permute-start | bytes 393224 | tf_op jit(solution)/shard_map/ppermute | solution.py:182
  16.5 11.5 %collective-permute-start.5 = (bf16[128,512]{1,0:T(8,128)(2,1)S(1)}, bf16[128,512]{1,0:T(8,128)(2,1)S(1)}, u32[]{:S(2)}, u32[]{:S(2)}) collective-permute-start(bf16[128,512]{1,0:T(8,128)(2,1)S(1)} %collective-permute-done.4.refs_4_.refs_2_), channel_id=1, source_target_pairs={{0,1},{1,0},{2,3},{3,2},{4,5},{5,4},{6,7},{7,6},{8,9},{9,8},{10,11... | collective-permute-start | bytes 393224 | tf_op jit(solution)/shard_map/ppermute | solution.py:182
  16.5 6.1 %collective-permute-start.8 = (bf16[128,256]{1,0:T(8,128)(2,1)S(1)}, bf16[128,256]{1,0:T(8,128)(2,1)S(1)}, u32[]{:S(2)}, u32[]{:S(2)}) collective-permute-start(bf16[128,256]{1,0:T(8,128)(2,1)S(1)} %get-tuple-element.11.refs_0_), channel_id=1, source_target_pairs={{0,24},{1,25},{2,26},{3,27},{4,28},{5,29},{6,30},{7,31},{8,0},{9,1... | collective-permute-start | bytes 196616 | tf_op jit(solution)/shard_map/ppermute | solution.py:182
  20.1 7.1 %collective-permute-start.7 = (bf16[128,256]{1,0:T(8,128)(2,1)S(1)}, bf16[128,256]{1,0:T(8,128)(2,1)S(1)}, u32[]{:S(2)}, u32[]{:S(2)}) collective-permute-start(bf16[128,256]{1,0:T(8,128)(2,1)S(1)} %get-tuple-element.11.refs_0_), channel_id=1, source_target_pairs={{0,16},{1,17},{2,18},{3,19},{4,20},{5,21},{6,22},{7,23},{8,24},{9,... | collective-permute-start | bytes 196616 | tf_op jit(solution)/shard_map/ppermute | solution.py:182
  20.1 11.0 %collective-permute-start = (bf16[128,256]{1,0:T(8,128)(2,1)S(1)}, bf16[128,256]{1,0:T(8,128)(2,1)S(1)}, u32[]{:S(2)}, u32[]{:S(2)}) collective-permute-start(bf16[128,256]{1,0:T(8,128)(2,1)S(1)} %get-tuple-element.11.refs_0_), channel_id=1, source_target_pairs={{0,8},{1,9},{2,10},{3,11},{4,12},{5,13},{6,14},{7,15},{8,16},{9,17... | collective-permute-start | bytes 196616 | tf_op jit(solution)/shard_map/ppermute | solution.py:182
  28.6 7.5 %collective-permute-start.9 = (bf16[136,256]{1,0:T(8,128)(2,1)S(1)}, bf16[136,256]{1,0:T(8,128)(2,1)S(1)}, u32[]{:S(2)}, u32[]{:S(2)}) collective-permute-start(bf16[136,256]{1,0:T(8,128)(2,1)S(1)} %get-tuple-element.18), channel_id=1, source_target_pairs={{0,16},{1,17},{2,18},{3,19},{4,20},{5,21},{6,22},{7,23},{8,24},{9,... | collective-permute-start | bytes 208904 | tf_op jit(solution)/shard_map/ppermute | solution.py:182
  28.8 7.3 %collective-permute-start.10 = (bf16[136,256]{1,0:T(8,128)(2,1)S(1)}, bf16[136,256]{1,0:T(8,128)(2,1)S(1)}, u32[]{:S(2)}, u32[]{:S(2)}) collective-permute-start(bf16[136,256]{1,0:T(8,128)(2,1)S(1)} %get-tuple-element.19), channel_id=1, source_target_pairs={{0,8},{1,9},{2,10},{3,11},{4,12},{5,13},{6,14},{7,15},{8,16},{9,17... | collective-permute-start | bytes 208904 | tf_op jit(solution)/shard_map/ppermute | solution.py:182
  32.0 5.2 %collective-permute-start.6 = (bf16[136,256]{1,0:T(8,128)(2,1)S(1)}, bf16[136,256]{1,0:T(8,128)(2,1)S(1)}, u32[]{:S(2)}, u32[]{:S(2)}) collective-permute-start(bf16[136,256]{1,0:T(8,128)(2,1)S(1)} %get-tuple-element.15), channel_id=1, source_target_pairs={{0,24},{1,25},{2,26},{3,27},{4,28},{5,29},{6,30},{7,31},{8,0},{9,1... | collective-permute-start | bytes 208904 | tf_op jit(solution)/shard_map/ppermute | solution.py:182

commit v3 on v2

--- a/solution.py
+++ b/solution.py
@@ -183,9 +183,11 @@
 
     nears = [kv] + [sent(kv, over_plane(s)) for s in range(1, plane)]
     queries = [q] + [sent(q, over_outer(s)) for s in range(1, outer)]
-    first = jnp.concatenate(nears[:-1], axis=0)
-    early = (first, sent(first, over_core))
-    late = (nears[-1], sent(nears[-1], over_core))
+    halves = [
+        jnp.concatenate(x, axis=0) for x in (nears[: plane // 2], nears[plane // 2 :])
+    ]
+    early = (halves[0], sent(halves[0], over_core))
+    late = (halves[1], sent(halves[1], over_core))
 
     f32 = jnp.float32
     part = jax.ShapeDtypeStruct((rows + TAIL, 2 * head), jnp.bfloat16)

time: 38.5 us -> 32.9 us (0.85)
  waiting for transfers between devices: 18.5 us -> 14.2 us
  starting transfers between devices: 14.8 us -> 13.9 us
    ppermute x11, waiting for transfers between devices: 18.5 us -> 14.2 us  [sent(): return lax.ppermute(x, axes, pairs)]
    ppermute x11, starting transfers between devices: 14.8 us -> 13.9 us  [sent(): return lax.ppermute(x, axes, pairs)]
  transfers between devices with their start and end apart: 11 -> 11, of which waited for: 7 -> 5; matrix products, arithmetic and copies ran while one was open for 0% -> 0% of each run, Pallas kernels for 6% -> 6%
where the time goes in v3:
time: 32.9 us; the launch traced here: 32.7 us
  waiting for transfers between devices  14.2 us (43%)
  starting transfers between devices  13.9 us (42%)
  Pallas kernels  3.9 us (12%)
  between operations  0.71 us (2%)
    ppermute x11, waiting for transfers between devices, sent(): return lax.ppermute(x, axes, pairs)  14.2 us
    ppermute x11, starting transfers between devices, sent(): return lax.ppermute(x, axes, pairs)  13.9 us
    pallas_call x3, Pallas kernels, panel(): pl.pallas_call(functools.partial(panel_kernel, scale, keeps, n, len(sides...  2 us
    pallas_call x1, Pallas kernels, on_device(): pl.pallas_call(merge_kernel, out_shape=(jax.ShapeDtypeStruct((rows, head)...  1 us
    pallas_call x1, Pallas kernels, on_device(): pl.pallas_call(pack_kernel, out_shape=(jax.ShapeDtypeStruct((rows, 4 * he...  0.89 us
  transfers between devices with their start and end apart: 11, of which 5 were waited for; matrix products, arithmetic and copies ran while one was open for 0% of the time, Pallas kernels for 6%

profile of v3, /device:TPU:0, one launch (start us, length us, event | category | flops | bytes accessed | tf_op | source)
XLA Modules:
  0.0 32.7 jit_solution(1017365078412902)
XLA Ops:
  0.6 0.9 %pack.1 = (bf16[128,512]{1,0:T(8,128)(2,1)S(1)}, bf16[128,256]{1,0:T(8,128)(2,1)S(1)}) custom-call(bf16[128,128]{1,0:T(8,128)(2,1)} %k.1, bf16[128,128]{1,0:T(8,128)(2,1)} %dk.1, bf16[128,128]{1,0:T(8,128)(2,1)} %v.1, bf16[128,128]{1,0:T(8,128)(2,1)} %dv.1, bf16[128,128]{1,0:T(8,128)(2,1)} %q.1, bf16[128,128]{1,0:T(8,128)(2,1)} %dq.1), custom_call_target="tpu_custom_call" | custom-call | tf_op jit(solution)/shard_map/pack/pallas_call | solution.py:163
  1.5 3.1 %collective-permute-start.1 = (bf16[128,512]{1,0:T(8,128)(2,1)S(1)}, bf16[128,512]{1,0:T(8,128)(2,1)S(1)}, u32[]{:S(2)}, u32[]{:S(2)}) collective-permute-start(bf16[128,512]{1,0:T(8,128)(2,1)S(1)} %get-tuple-element.12), channel_id=1, source_target_pairs={{0,2},{1,3},{2,0},{3,1},{4,6},{5,7},{6,4},{7,5},{8,10},{9,11},{10,... | collective-permute-start | bytes 393224 | tf_op jit(solution)/shard_map/ppermute | solution.py:182
  4.6 1.4 %collective-permute-start.4 = (bf16[128,512]{1,0:T(8,128)(2,1)S(1)}, bf16[128,512]{1,0:T(8,128)(2,1)S(1)}, u32[]{:S(2)}, u32[]{:S(2)}) collective-permute-start(bf16[128,512]{1,0:T(8,128)(2,1)S(1)} %get-tuple-element.12), channel_id=1, source_target_pairs={{0,6},{1,7},{2,4},{3,5},{4,2},{5,3},{6,0},{7,1},{8,14},{9,15},{10,... | collective-permute-start | bytes 393224 | tf_op jit(solution)/shard_map/ppermute | solution.py:182
  6.0 0.1 collective-permute-start.3
  6.1 4.0 %collective-permute-done.1 = bf16[128,512]{1,0:T(8,128)(2,1)S(1)} collective-permute-done((bf16[128,512]{1,0:T(8,128)(2,1)S(1)}, bf16[128,512]{1,0:T(8,128)(2,1)S(1)}, u32[]{:S(2)}, u32[]{:S(2)}) %collective-permute-start.1) | collective-permute-done | bytes 131104 | tf_op jit(solution)/shard_map/ppermute | solution.py:182
  10.2 0.1 collective-permute-start.2
  10.2 2.0 %collective-permute-done.3 = bf16[128,512]{1,0:T(8,128)(2,1)S(1)} collective-permute-done((bf16[128,512]{1,0:T(8,128)(2,1)S(1)}, bf16[128,512]{1,0:T(8,128)(2,1)S(1)}, u32[]{:S(2)}, u32[]{:S(2)}) %collective-permute-start.3) | collective-permute-done | bytes 131104 | tf_op jit(solution)/shard_map/ppermute | solution.py:182
  12.2 0.0 collective-permute-done.4
  12.2 0.1 collective-permute-start.5
  12.3 1.8 %collective-permute-start = (bf16[128,256]{1,0:T(8,128)(2,1)S(1)}, bf16[128,256]{1,0:T(8,128)(2,1)S(1)}, u32[]{:S(2)}, u32[]{:S(2)}) collective-permute-start(bf16[128,256]{1,0:T(8,128)(2,1)S(1)} %get-tuple-element.11.refs_0_), channel_id=1, source_target_pairs={{0,8},{1,9},{2,10},{3,11},{4,12},{5,13},{6,14},{7,15},{8,16},{9,17... | collective-permute-start | bytes 196616 | tf_op jit(solution)/shard_map/ppermute | solution.py:182
  14.1 2.1 %collective-permute-start.8 = (bf16[128,256]{1,0:T(8,128)(2,1)S(1)}, bf16[128,256]{1,0:T(8,128)(2,1)S(1)}, u32[]{:S(2)}, u32[]{:S(2)}) collective-permute-start(bf16[128,256]{1,0:T(8,128)(2,1)S(1)} %get-tuple-element.11.refs_0_), channel_id=1, source_target_pairs={{0,24},{1,25},{2,26},{3,27},{4,28},{5,29},{6,30},{7,31},{8,0},{9,1... | collective-permute-start | bytes 196616 | tf_op jit(solution)/shard_map/ppermute | solution.py:182
  16.2 0.9 %collective-permute-start.7 = (bf16[128,256]{1,0:T(8,128)(2,1)S(1)}, bf16[128,256]{1,0:T(8,128)(2,1)S(1)}, u32[]{:S(2)}, u32[]{:S(2)}) collective-permute-start(bf16[128,256]{1,0:T(8,128)(2,1)S(1)} %get-tuple-element.11.refs_0_), channel_id=1, source_target_pairs={{0,16},{1,17},{2,18},{3,19},{4,20},{5,21},{6,22},{7,23},{8,24},{9,... | collective-permute-start | bytes 196616 | tf_op jit(solution)/shard_map/ppermute | solution.py:182
  17.1 1.8 %collective-permute-done.refs_1_ = bf16[128,256]{1,0:T(8,128)(2,1)S(1)} collective-permute-done((bf16[128,256]{1,0:T(8,128)(2,1)S(1)}, bf16[128,256]{1,0:T(8,128)(2,1)S(1)}, u32[]{:S(2)}, u32[]{:S(2)}) %collective-permute-start) | collective-permute-done | bytes 65568 | tf_op jit(solution)/shard_map/ppermute | solution.py:182
  18.9 0.0 collective-permute-done.2.refs_3_
  18.9 0.0 collective-permute-done.5.refs_5_.refs_3_
  18.9 0.9 %shard_map.77 = (f32[128,256]{1,0:T(8,128)S(1)}, f32[8,128]{1,0:T(8,128)S(1)}, bf16[136,256]{1,0:T(8,128)(2,1)S(1)}) custom-call(bf16[128,256]{1,0:T(8,128)(2,1)S(1)} %get-tuple-element.11.refs_0_, bf16[128,256]{1,0:T(8,128)(2,1)S(1)} %collective-permute-done.refs_1_, bf16[256,512]{1,0:T(8,128)(2,1)S(1)} %constant_dynamic-update-slice_fusion.refs_2_, ...), custom_call_target="tpu_custom_call" | custom-call | flops 671088640 | tf_op jit(solution)/shard_map/pallas_call | solution.py:211
  19.8 1.7 %collective-permute-start.6 = (bf16[136,256]{1,0:T(8,128)(2,1)S(1)}, bf16[136,256]{1,0:T(8,128)(2,1)S(1)}, u32[]{:S(2)}, u32[]{:S(2)}) collective-permute-start(bf16[136,256]{1,0:T(8,128)(2,1)S(1)} %get-tuple-element.15), channel_id=1, source_target_pairs={{0,24},{1,25},{2,26},{3,27},{4,28},{5,29},{6,30},{7,31},{8,0},{9,1... | collective-permute-start | bytes 208904 | tf_op jit(solution)/shard_map/ppermute | solution.py:182
  21.5 0.0 collective-permute-done.8.refs_1_
  21.5 1.7 %collective-permute-done.7.refs_0_ = bf16[128,256]{1,0:T(8,128)(2,1)S(1)} collective-permute-done((bf16[128,256]{1,0:T(8,128)(2,1)S(1)}, bf16[128,256]{1,0:T(8,128)(2,1)S(1)}, u32[]{:S(2)}, u32[]{:S(2)}) %collective-permute-start.7) | collective-permute-done | bytes 65568 | tf_op jit(solution)/shard_map/ppermute | solution.py:182
  23.1 0.6 %shard_map.78 = (f32[256,384]{1,0:T(8,128)S(1)}, f32[256,384]{1,0:T(8,128)S(1)}) custom-call(bf16[128,256]{1,0:T(8,128)(2,1)S(1)} %collective-permute-done.7.refs_0_, bf16[128,256]{1,0:T(8,128)(2,1)S(1)} %collective-permute-done.8.refs_1_, bf16[256,512]{1,0:T(8,128)(2,1)S(1)} %constant_dynamic-update-slice_fusion.refs_2_, ...), custom_call_target="tpu_custom_call" | custom-call | flops 335544320 | tf_op jit(solution)/shard_map/pallas_call | solution.py:211
  23.7 0.6 %shard_map.79 = (bf16[136,256]{1,0:T(8,128)(2,1)S(1)}, bf16[136,256]{1,0:T(8,128)(2,1)S(1)}) custom-call(bf16[128,256]{1,0:T(8,128)(2,1)S(1)} %collective-permute-done.7.refs_0_, bf16[128,256]{1,0:T(8,128)(2,1)S(1)} %collective-permute-done.8.refs_1_, bf16[256,512]{1,0:T(8,128)(2,1)S(1)} %constant_dynamic-update-slice_fusion.2.refs_4_.refs_2_, ...), custom_call_target="tpu_custom_call" | custom-call | flops 335544320 | tf_op jit(solution)/shard_map/pallas_call | solution.py:211
  24.3 0.1 collective-permute-start.9
  24.4 2.6 %collective-permute-start.10 = (bf16[136,256]{1,0:T(8,128)(2,1)S(1)}, bf16[136,256]{1,0:T(8,128)(2,1)S(1)}, u32[]{:S(2)}, u32[]{:S(2)}) collective-permute-start(bf16[136,256]{1,0:T(8,128)(2,1)S(1)} %get-tuple-element.19), channel_id=1, source_target_pairs={{0,8},{1,9},{2,10},{3,11},{4,12},{5,13},{6,14},{7,15},{8,16},{9,17... | collective-permute-start | bytes 208904 | tf_op jit(solution)/shard_map/ppermute | solution.py:182
  27.0 0.0 collective-permute-done.6.refs_0_
  27.0 4.8 %collective-permute-done.9.refs_1_ = bf16[136,256]{1,0:T(8,128)(2,1)S(1)} collective-permute-done((bf16[136,256]{1,0:T(8,128)(2,1)S(1)}, bf16[136,256]{1,0:T(8,128)(2,1)S(1)}, u32[]{:S(2)}, u32[]{:S(2)}) %collective-permute-start.9) | collective-permute-done | bytes 69664 | tf_op jit(solution)/shard_map/ppermute | solution.py:182
  31.7 0.0 collective-permute-done.10.refs_2_
  31.7 1.0 %merge.1 = (f32[128,128]{1,0:T(8,128)}, f32[128,128]{1,0:T(8,128)}) custom-call(f32[128,256]{1,0:T(8,128)S(1)} %get-tuple-element.13.own_ref, f32[8,128]{1,0:T(8,128)S(1)} %get-tuple-element.14.stat_ref, bf16[136,256]{1,0:T(8,128)(2,1)S(1)} %collective-permute-done.6.refs_0_, bf16[136,256]{1,0:T(8,128)(2,1)S(1)} %collective-permute-done.9.refs_1_, ...), custom_call_target="tpu_custom_call" | custom-call | tf_op jit(solution)/shard_map/merge/pallas_call | solution.py:229
  (4 shorter events, 0.0 us)
Async XLA Ops:
  1.5 8.6 %collective-permute-start.1 = (bf16[128,512]{1,0:T(8,128)(2,1)S(1)}, bf16[128,512]{1,0:T(8,128)(2,1)S(1)}, u32[]{:S(2)}, u32[]{:S(2)}) collective-permute-start(bf16[128,512]{1,0:T(8,128)(2,1)S(1)} %get-tuple-element.12), channel_id=1, source_target_pairs={{0,2},{1,3},{2,0},{3,1},{4,6},{5,7},{6,4},{7,5},{8,10},{9,11},{10,... | collective-permute-start | bytes 393224 | tf_op jit(solution)/shard_map/ppermute | solution.py:182
  4.6 7.6 %collective-permute-start.4 = (bf16[128,512]{1,0:T(8,128)(2,1)S(1)}, bf16[128,512]{1,0:T(8,128)(2,1)S(1)}, u32[]{:S(2)}, u32[]{:S(2)}) collective-permute-start(bf16[128,512]{1,0:T(8,128)(2,1)S(1)} %get-tuple-element.12), channel_id=1, source_target_pairs={{0,6},{1,7},{2,4},{3,5},{4,2},{5,3},{6,0},{7,1},{8,14},{9,15},{10,... | collective-permute-start | bytes 393224 | tf_op jit(solution)/shard_map/ppermute | solution.py:182
  6.0 6.2 %collective-permute-start.3 = (bf16[128,512]{1,0:T(8,128)(2,1)S(1)}, bf16[128,512]{1,0:T(8,128)(2,1)S(1)}, u32[]{:S(2)}, u32[]{:S(2)}) collective-permute-start(bf16[128,512]{1,0:T(8,128)(2,1)S(1)} %get-tuple-element.12), channel_id=1, source_target_pairs={{0,4},{1,5},{2,6},{3,7},{4,0},{5,1},{6,2},{7,3},{8,12},{9,13},{10,... | collective-permute-start | bytes 393224 | tf_op jit(solution)/shard_map/ppermute | solution.py:182
  10.2 8.8 %collective-permute-start.2 = (bf16[256,512]{1,0:T(8,128)(2,1)S(1)}, bf16[256,512]{1,0:T(8,128)(2,1)S(1)}, u32[]{:S(2)}, u32[]{:S(2)}) collective-permute-start(bf16[256,512]{1,0:T(8,128)(2,1)S(1)} %constant_dynamic-update-slice_fusion.refs_2_), channel_id=1, source_target_pairs={{0,1},{1,0},{2,3},{3,2},{4,5},{5,4},{6,7},{7,6},{8,9},{9,8},{10,11... | collective-permute-start | bytes 786440 | tf_op jit(solution)/shard_map/ppermute | solution.py:182
  12.2 6.7 %collective-permute-start.5 = (bf16[256,512]{1,0:T(8,128)(2,1)S(1)}, bf16[256,512]{1,0:T(8,128)(2,1)S(1)}, u32[]{:S(2)}, u32[]{:S(2)}) collective-permute-start(bf16[256,512]{1,0:T(8,128)(2,1)S(1)} %constant_dynamic-update-slice_fusion.2.refs_4_.refs_2_), channel_id=1, source_target_pairs={{0,1},{1,0},{2,3},{3,2},{4,5},{5,4},{6,7},{7,6},{8,9},{9,8},{10,11... | collective-permute-start | bytes 786440 | tf_op jit(solution)/shard_map/ppermute | solution.py:182
  12.3 6.6 %collective-permute-start = (bf16[128,256]{1,0:T(8,128)(2,1)S(1)}, bf16[128,256]{1,0:T(8,128)(2,1)S(1)}, u32[]{:S(2)}, u32[]{:S(2)}) collective-permute-start(bf16[128,256]{1,0:T(8,128)(2,1)S(1)} %get-tuple-element.11.refs_0_), channel_id=1, source_target_pairs={{0,8},{1,9},{2,10},{3,11},{4,12},{5,13},{6,14},{7,15},{8,16},{9,17... | collective-permute-start | bytes 196616 | tf_op jit(solution)/shard_map/ppermute | solution.py:182
  14.1 7.4 %collective-permute-start.8 = (bf16[128,256]{1,0:T(8,128)(2,1)S(1)}, bf16[128,256]{1,0:T(8,128)(2,1)S(1)}, u32[]{:S(2)}, u32[]{:S(2)}) collective-permute-start(bf16[128,256]{1,0:T(8,128)(2,1)S(1)} %get-tuple-element.11.refs_0_), channel_id=1, source_target_pairs={{0,24},{1,25},{2,26},{3,27},{4,28},{5,29},{6,30},{7,31},{8,0},{9,1... | collective-permute-start | bytes 196616 | tf_op jit(solution)/shard_map/ppermute | solution.py:182
  16.2 6.9 %collective-permute-start.7 = (bf16[128,256]{1,0:T(8,128)(2,1)S(1)}, bf16[128,256]{1,0:T(8,128)(2,1)S(1)}, u32[]{:S(2)}, u32[]{:S(2)}) collective-permute-start(bf16[128,256]{1,0:T(8,128)(2,1)S(1)} %get-tuple-element.11.refs_0_), channel_id=1, source_target_pairs={{0,16},{1,17},{2,18},{3,19},{4,20},{5,21},{6,22},{7,23},{8,24},{9,... | collective-permute-start | bytes 196616 | tf_op jit(solution)/shard_map/ppermute | solution.py:182
  19.8 7.2 %collective-permute-start.6 = (bf16[136,256]{1,0:T(8,128)(2,1)S(1)}, bf16[136,256]{1,0:T(8,128)(2,1)S(1)}, u32[]{:S(2)}, u32[]{:S(2)}) collective-permute-start(bf16[136,256]{1,0:T(8,128)(2,1)S(1)} %get-tuple-element.15), channel_id=1, source_target_pairs={{0,24},{1,25},{2,26},{3,27},{4,28},{5,29},{6,30},{7,31},{8,0},{9,1... | collective-permute-start | bytes 208904 | tf_op jit(solution)/shard_map/ppermute | solution.py:182
  24.3 7.5 %collective-permute-start.9 = (bf16[136,256]{1,0:T(8,128)(2,1)S(1)}, bf16[136,256]{1,0:T(8,128)(2,1)S(1)}, u32[]{:S(2)}, u32[]{:S(2)}) collective-permute-start(bf16[136,256]{1,0:T(8,128)(2,1)S(1)} %get-tuple-element.18), channel_id=1, source_target_pairs={{0,16},{1,17},{2,18},{3,19},{4,20},{5,21},{6,22},{7,23},{8,24},{9,... | collective-permute-start | bytes 208904 | tf_op jit(solution)/shard_map/ppermute | solution.py:182
  24.4 7.4 %collective-permute-start.10 = (bf16[136,256]{1,0:T(8,128)(2,1)S(1)}, bf16[136,256]{1,0:T(8,128)(2,1)S(1)}, u32[]{:S(2)}, u32[]{:S(2)}) collective-permute-start(bf16[136,256]{1,0:T(8,128)(2,1)S(1)} %get-tuple-element.19), channel_id=1, source_target_pairs={{0,8},{1,9},{2,10},{3,11},{4,12},{5,13},{6,14},{7,15},{8,16},{9,17... | collective-permute-start | bytes 208904 | tf_op jit(solution)/shard_map/ppermute | solution.py:182

commit v4 on v2

--- a/solution.py
+++ b/solution.py
@@ -155,7 +155,10 @@
         return (o * plane + p) * cores + c
 
     every = [(o, p, c) for o in range(outer) for p in range(plane) for c in range(cores)]
-    over_plane = lambda s: [(index(o, p, c), index(o, mix(p, s, plane), c)) for o, p, c in every]
+    turn = lambda s, c: 1 + (s - 1 + c) % (plane - 1)
+    over_plane = lambda s: [
+        (index(o, p, c), index(o, mix(p, turn(s, c), plane), c)) for o, p, c in every
+    ]
     over_core = [(index(o, p, c), index(o, p, (c + 1) % cores)) for o, p, c in every]
     over_outer = lambda s: [(index(o, p, c), index((o + s) % outer, p, c)) for o, p, c in every]
     outer_back = lambda s: over_outer(outer - s)

time: 38.5 us -> 38.5 us (level)
  no operation moved by 1% of the time
where the time goes in v4:
time: 38.5 us; the launch traced here: 38.3 us
  waiting for transfers between devices  18.3 us (48%)
  starting transfers between devices  15.1 us (39%)
  Pallas kernels  4.21 us (11%)
  between operations  0.68 us (2%)
    ppermute x11, waiting for transfers between devices, sent(): return lax.ppermute(x, axes, pairs)  18.3 us
    ppermute x11, starting transfers between devices, sent(): return lax.ppermute(x, axes, pairs)  15.1 us
    pallas_call x3, Pallas kernels, panel(): pl.pallas_call(functools.partial(panel_kernel, scale, keeps, n, len(sides...  2.32 us
    pallas_call x1, Pallas kernels, on_device(): pl.pallas_call(merge_kernel, out_shape=(jax.ShapeDtypeStruct((rows, head)...  1 us
    pallas_call x1, Pallas kernels, on_device(): pl.pallas_call(pack_kernel, out_shape=(jax.ShapeDtypeStruct((rows, 4 * he...  0.89 us
  transfers between devices with their start and end apart: 11, of which 7 were waited for; matrix products, arithmetic and copies ran while one was open for 0% of the time, Pallas kernels for 6%

profile of v4, /device:TPU:0, one launch (start us, length us, event | category | flops | bytes accessed | tf_op | source)
XLA Modules:
  0.0 38.3 jit_solution(8298842220864840829)
XLA Ops:
  0.6 0.9 %pack.1 = (bf16[128,512]{1,0:T(8,128)(2,1)S(1)}, bf16[128,256]{1,0:T(8,128)(2,1)S(1)}) custom-call(bf16[128,128]{1,0:T(8,128)(2,1)} %k.1, bf16[128,128]{1,0:T(8,128)(2,1)} %dk.1, bf16[128,128]{1,0:T(8,128)(2,1)} %v.1, bf16[128,128]{1,0:T(8,128)(2,1)} %dv.1, bf16[128,128]{1,0:T(8,128)(2,1)} %q.1, bf16[128,128]{1,0:T(8,128)(2,1)} %dq.1), custom_call_target="tpu_custom_call" | custom-call | tf_op jit(solution)/shard_map/pack/pallas_call | solution.py:166
  1.5 3.1 %collective-permute-start.1 = (bf16[128,512]{1,0:T(8,128)(2,1)S(1)}, bf16[128,512]{1,0:T(8,128)(2,1)S(1)}, u32[]{:S(2)}, u32[]{:S(2)}) collective-permute-start(bf16[128,512]{1,0:T(8,128)(2,1)S(1)} %get-tuple-element.12), channel_id=1, source_target_pairs={{0,2},{1,5},{2,0},{3,7},{4,6},{5,1},{6,4},{7,3},{8,10},{9,13},{10,... | collective-permute-start | bytes 393224 | tf_op jit(solution)/shard_map/ppermute | solution.py:185
  4.6 1.5 %collective-permute-start.2 = (bf16[128,512]{1,0:T(8,128)(2,1)S(1)}, bf16[128,512]{1,0:T(8,128)(2,1)S(1)}, u32[]{:S(2)}, u32[]{:S(2)}) collective-permute-start(bf16[128,512]{1,0:T(8,128)(2,1)S(1)} %get-tuple-element.12), channel_id=1, source_target_pairs={{0,4},{1,7},{2,6},{3,5},{4,0},{5,3},{6,2},{7,1},{8,12},{9,15},{10,... | collective-permute-start | bytes 393224 | tf_op jit(solution)/shard_map/ppermute | solution.py:185
  6.1 1.8 %collective-permute-done.1 = bf16[128,512]{1,0:T(8,128)(2,1)S(1)} collective-permute-done((bf16[128,512]{1,0:T(8,128)(2,1)S(1)}, bf16[128,512]{1,0:T(8,128)(2,1)S(1)}, u32[]{:S(2)}, u32[]{:S(2)}) %collective-permute-start.1) | collective-permute-done | bytes 131104 | tf_op jit(solution)/shard_map/ppermute | solution.py:185
  7.9 2.6 %collective-permute-done.2 = bf16[128,512]{1,0:T(8,128)(2,1)S(1)} collective-permute-done((bf16[128,512]{1,0:T(8,128)(2,1)S(1)}, bf16[128,512]{1,0:T(8,128)(2,1)S(1)}, u32[]{:S(2)}, u32[]{:S(2)}) %collective-permute-start.2) | collective-permute-done | bytes 131104 | tf_op jit(solution)/shard_map/ppermute | solution.py:185
  10.5 0.1 collective-permute-start.3
  10.6 1.7 %collective-permute-start.4 = (bf16[128,512]{1,0:T(8,128)(2,1)S(1)}, bf16[128,512]{1,0:T(8,128)(2,1)S(1)}, u32[]{:S(2)}, u32[]{:S(2)}) collective-permute-start(bf16[128,512]{1,0:T(8,128)(2,1)S(1)} %get-tuple-element.12), channel_id=1, source_target_pairs={{0,6},{1,3},{2,4},{3,1},{4,2},{5,7},{6,0},{7,5},{8,14},{9,11},{10,... | collective-permute-start | bytes 393224 | tf_op jit(solution)/shard_map/ppermute | solution.py:185
  12.3 4.2 %collective-permute-done.4.refs_4_.refs_2_ = bf16[128,512]{1,0:T(8,128)(2,1)S(1)} collective-permute-done((bf16[128,512]{1,0:T(8,128)(2,1)S(1)}, bf16[128,512]{1,0:T(8,128)(2,1)S(1)}, u32[]{:S(2)}, u32[]{:S(2)}) %collective-permute-start.4) | collective-permute-done | bytes 131104 | tf_op jit(solution)/shard_map/ppermute | solution.py:185
  16.5 0.0 collective-permute-start.5
  16.5 3.6 %collective-permute-start.8 = (bf16[128,256]{1,0:T(8,128)(2,1)S(1)}, bf16[128,256]{1,0:T(8,128)(2,1)S(1)}, u32[]{:S(2)}, u32[]{:S(2)}) collective-permute-start(bf16[128,256]{1,0:T(8,128)(2,1)S(1)} %get-tuple-element.11.refs_0_), channel_id=1, source_target_pairs={{0,24},{1,25},{2,26},{3,27},{4,28},{5,29},{6,30},{7,31},{8,0},{9,1... | collective-permute-start | bytes 196616 | tf_op jit(solution)/shard_map/ppermute | solution.py:185
  20.1 0.0 collective-permute-start.7
  20.1 1.0 %collective-permute-start = (bf16[128,256]{1,0:T(8,128)(2,1)S(1)}, bf16[128,256]{1,0:T(8,128)(2,1)S(1)}, u32[]{:S(2)}, u32[]{:S(2)}) collective-permute-start(bf16[128,256]{1,0:T(8,128)(2,1)S(1)} %get-tuple-element.11.refs_0_), channel_id=1, source_target_pairs={{0,8},{1,9},{2,10},{3,11},{4,12},{5,13},{6,14},{7,15},{8,16},{9,17... | collective-permute-start | bytes 196616 | tf_op jit(solution)/shard_map/ppermute | solution.py:185
  21.1 1.5 %collective-permute-done.8.refs_1_ = bf16[128,256]{1,0:T(8,128)(2,1)S(1)} collective-permute-done((bf16[128,256]{1,0:T(8,128)(2,1)S(1)}, bf16[128,256]{1,0:T(8,128)(2,1)S(1)}, u32[]{:S(2)}, u32[]{:S(2)}) %collective-permute-start.8) | collective-permute-done | bytes 65568 | tf_op jit(solution)/shard_map/ppermute | solution.py:185
  22.6 4.6 %collective-permute-done.7.refs_0_ = bf16[128,256]{1,0:T(8,128)(2,1)S(1)} collective-permute-done((bf16[128,256]{1,0:T(8,128)(2,1)S(1)}, bf16[128,256]{1,0:T(8,128)(2,1)S(1)}, u32[]{:S(2)}, u32[]{:S(2)}) %collective-permute-start.7) | collective-permute-done | bytes 65568 | tf_op jit(solution)/shard_map/ppermute | solution.py:185
  27.2 0.0 collective-permute-done.3.refs_3_
  27.3 0.8 %shard_map.78 = (f32[256,384]{1,0:T(8,128)S(1)}, f32[256,384]{1,0:T(8,128)S(1)}) custom-call(bf16[128,256]{1,0:T(8,128)(2,1)S(1)} %collective-permute-done.7.refs_0_, bf16[128,256]{1,0:T(8,128)(2,1)S(1)} %collective-permute-done.8.refs_1_, bf16[384,512]{1,0:T(8,128)(2,1)S(1)} %constant_dynamic-update-slice_fusion.refs_2_, ...), custom_call_target="tpu_custom_call" | custom-call | flops 503316480 | tf_op jit(solution)/shard_map/pallas_call | solution.py:212
  28.0 0.0 collective-permute-done.5.refs_5_.refs_3_
  28.1 0.6 %shard_map.79 = (bf16[136,256]{1,0:T(8,128)(2,1)S(1)}, bf16[136,256]{1,0:T(8,128)(2,1)S(1)}) custom-call(bf16[128,256]{1,0:T(8,128)(2,1)S(1)} %collective-permute-done.7.refs_0_, bf16[128,256]{1,0:T(8,128)(2,1)S(1)} %collective-permute-done.8.refs_1_, bf16[128,512]{1,0:T(8,128)(2,1)S(1)} %collective-permute-done.4.refs_4_.refs_2_, ...), custom_call_target="tpu_custom_call" | custom-call | flops 167772160 | tf_op jit(solution)/shard_map/pallas_call | solution.py:212
  28.6 0.2 collective-permute-start.9
  28.9 2.3 %collective-permute-start.10 = (bf16[136,256]{1,0:T(8,128)(2,1)S(1)}, bf16[136,256]{1,0:T(8,128)(2,1)S(1)}, u32[]{:S(2)}, u32[]{:S(2)}) collective-permute-start(bf16[136,256]{1,0:T(8,128)(2,1)S(1)} %get-tuple-element.19), channel_id=1, source_target_pairs={{0,8},{1,9},{2,10},{3,11},{4,12},{5,13},{6,14},{7,15},{8,16},{9,17... | collective-permute-start | bytes 208904 | tf_op jit(solution)/shard_map/ppermute | solution.py:185
  31.1 0.0 collective-permute-done.refs_1_
  31.1 0.9 %shard_map.77 = (f32[128,256]{1,0:T(8,128)S(1)}, f32[8,128]{1,0:T(8,128)S(1)}, bf16[136,256]{1,0:T(8,128)(2,1)S(1)}) custom-call(bf16[128,256]{1,0:T(8,128)(2,1)S(1)} %get-tuple-element.11.refs_0_, bf16[128,256]{1,0:T(8,128)(2,1)S(1)} %collective-permute-done.refs_1_, bf16[384,512]{1,0:T(8,128)(2,1)S(1)} %constant_dynamic-update-slice_fusion.refs_2_, ...), custom_call_target="tpu_custom_call" | custom-call | flops 671088640 | tf_op jit(solution)/shard_map/pallas_call | solution.py:212
  32.1 1.6 %collective-permute-start.6 = (bf16[136,256]{1,0:T(8,128)(2,1)S(1)}, bf16[136,256]{1,0:T(8,128)(2,1)S(1)}, u32[]{:S(2)}, u32[]{:S(2)}) collective-permute-start(bf16[136,256]{1,0:T(8,128)(2,1)S(1)} %get-tuple-element.15), channel_id=1, source_target_pairs={{0,24},{1,25},{2,26},{3,27},{4,28},{5,29},{6,30},{7,31},{8,0},{9,1... | collective-permute-start | bytes 208904 | tf_op jit(solution)/shard_map/ppermute | solution.py:185
  33.7 2.5 %collective-permute-done.9.refs_1_ = bf16[136,256]{1,0:T(8,128)(2,1)S(1)} collective-permute-done((bf16[136,256]{1,0:T(8,128)(2,1)S(1)}, bf16[136,256]{1,0:T(8,128)(2,1)S(1)}, u32[]{:S(2)}, u32[]{:S(2)}) %collective-permute-start.9) | collective-permute-done | bytes 69664 | tf_op jit(solution)/shard_map/ppermute | solution.py:185
  36.2 0.0 collective-permute-done.10.refs_2_
  36.2 1.2 %collective-permute-done.6.refs_0_ = bf16[136,256]{1,0:T(8,128)(2,1)S(1)} collective-permute-done((bf16[136,256]{1,0:T(8,128)(2,1)S(1)}, bf16[136,256]{1,0:T(8,128)(2,1)S(1)}, u32[]{:S(2)}, u32[]{:S(2)}) %collective-permute-start.6) | collective-permute-done | bytes 69664 | tf_op jit(solution)/shard_map/ppermute | solution.py:185
  37.3 1.0 %merge.1 = (f32[128,128]{1,0:T(8,128)}, f32[128,128]{1,0:T(8,128)}) custom-call(f32[128,256]{1,0:T(8,128)S(1)} %get-tuple-element.13.own_ref, f32[8,128]{1,0:T(8,128)S(1)} %get-tuple-element.14.stat_ref, bf16[136,256]{1,0:T(8,128)(2,1)S(1)} %collective-permute-done.6.refs_0_, bf16[136,256]{1,0:T(8,128)(2,1)S(1)} %collective-permute-done.9.refs_1_, ...), custom_call_target="tpu_custom_call" | custom-call | tf_op jit(solution)/shard_map/merge/pallas_call | solution.py:230
  (3 shorter events, 0.0 us)
Async XLA Ops:
  1.5 6.3 %collective-permute-start.1 = (bf16[128,512]{1,0:T(8,128)(2,1)S(1)}, bf16[128,512]{1,0:T(8,128)(2,1)S(1)}, u32[]{:S(2)}, u32[]{:S(2)}) collective-permute-start(bf16[128,512]{1,0:T(8,128)(2,1)S(1)} %get-tuple-element.12), channel_id=1, source_target_pairs={{0,2},{1,5},{2,0},{3,7},{4,6},{5,1},{6,4},{7,3},{8,10},{9,13},{10,... | collective-permute-start | bytes 393224 | tf_op jit(solution)/shard_map/ppermute | solution.py:185
  4.6 5.9 %collective-permute-start.2 = (bf16[128,512]{1,0:T(8,128)(2,1)S(1)}, bf16[128,512]{1,0:T(8,128)(2,1)S(1)}, u32[]{:S(2)}, u32[]{:S(2)}) collective-permute-start(bf16[128,512]{1,0:T(8,128)(2,1)S(1)} %get-tuple-element.12), channel_id=1, source_target_pairs={{0,4},{1,7},{2,6},{3,5},{4,0},{5,3},{6,2},{7,1},{8,12},{9,15},{10,... | collective-permute-start | bytes 393224 | tf_op jit(solution)/shard_map/ppermute | solution.py:185
  10.5 16.8 %collective-permute-start.3 = (bf16[384,512]{1,0:T(8,128)(2,1)S(1)}, bf16[384,512]{1,0:T(8,128)(2,1)S(1)}, u32[]{:S(2)}, u32[]{:S(2)}) collective-permute-start(bf16[384,512]{1,0:T(8,128)(2,1)S(1)} %constant_dynamic-update-slice_fusion.refs_2_), channel_id=1, source_target_pairs={{0,1},{1,0},{2,3},{3,2},{4,5},{5,4},{6,7},{7,6},{8,9},{9,8},{10,11... | collective-permute-start | bytes 1179656 | tf_op jit(solution)/shard_map/ppermute | solution.py:185
  10.6 5.9 %collective-permute-start.4 = (bf16[128,512]{1,0:T(8,128)(2,1)S(1)}, bf16[128,512]{1,0:T(8,128)(2,1)S(1)}, u32[]{:S(2)}, u32[]{:S(2)}) collective-permute-start(bf16[128,512]{1,0:T(8,128)(2,1)S(1)} %get-tuple-element.12), channel_id=1, source_target_pairs={{0,6},{1,3},{2,4},{3,1},{4,2},{5,7},{6,0},{7,5},{8,14},{9,11},{10,... | collective-permute-start | bytes 393224 | tf_op jit(solution)/shard_map/ppermute | solution.py:185
  16.5 11.5 %collective-permute-start.5 = (bf16[128,512]{1,0:T(8,128)(2,1)S(1)}, bf16[128,512]{1,0:T(8,128)(2,1)S(1)}, u32[]{:S(2)}, u32[]{:S(2)}) collective-permute-start(bf16[128,512]{1,0:T(8,128)(2,1)S(1)} %collective-permute-done.4.refs_4_.refs_2_), channel_id=1, source_target_pairs={{0,1},{1,0},{2,3},{3,2},{4,5},{5,4},{6,7},{7,6},{8,9},{9,8},{10,11... | collective-permute-start | bytes 393224 | tf_op jit(solution)/shard_map/ppermute | solution.py:185
  16.5 6.1 %collective-permute-start.8 = (bf16[128,256]{1,0:T(8,128)(2,1)S(1)}, bf16[128,256]{1,0:T(8,128)(2,1)S(1)}, u32[]{:S(2)}, u32[]{:S(2)}) collective-permute-start(bf16[128,256]{1,0:T(8,128)(2,1)S(1)} %get-tuple-element.11.refs_0_), channel_id=1, source_target_pairs={{0,24},{1,25},{2,26},{3,27},{4,28},{5,29},{6,30},{7,31},{8,0},{9,1... | collective-permute-start | bytes 196616 | tf_op jit(solution)/shard_map/ppermute | solution.py:185
  20.1 7.1 %collective-permute-start.7 = (bf16[128,256]{1,0:T(8,128)(2,1)S(1)}, bf16[128,256]{1,0:T(8,128)(2,1)S(1)}, u32[]{:S(2)}, u32[]{:S(2)}) collective-permute-start(bf16[128,256]{1,0:T(8,128)(2,1)S(1)} %get-tuple-element.11.refs_0_), channel_id=1, source_target_pairs={{0,16},{1,17},{2,18},{3,19},{4,20},{5,21},{6,22},{7,23},{8,24},{9,... | collective-permute-start | bytes 196616 | tf_op jit(solution)/shard_map/ppermute | solution.py:185
  20.1 11.0 %collective-permute-start = (bf16[128,256]{1,0:T(8,128)(2,1)S(1)}, bf16[128,256]{1,0:T(8,128)(2,1)S(1)}, u32[]{:S(2)}, u32[]{:S(2)}) collective-permute-start(bf16[128,256]{1,0:T(8,128)(2,1)S(1)} %get-tuple-element.11.refs_0_), channel_id=1, source_target_pairs={{0,8},{1,9},{2,10},{3,11},{4,12},{5,13},{6,14},{7,15},{8,16},{9,17... | collective-permute-start | bytes 196616 | tf_op jit(solution)/shard_map/ppermute | solution.py:185
  28.6 7.5 %collective-permute-start.9 = (bf16[136,256]{1,0:T(8,128)(2,1)S(1)}, bf16[136,256]{1,0:T(8,128)(2,1)S(1)}, u32[]{:S(2)}, u32[]{:S(2)}) collective-permute-start(bf16[136,256]{1,0:T(8,128)(2,1)S(1)} %get-tuple-element.18), channel_id=1, source_target_pairs={{0,16},{1,17},{2,18},{3,19},{4,20},{5,21},{6,22},{7,23},{8,24},{9,... | collective-permute-start | bytes 208904 | tf_op jit(solution)/shard_map/ppermute | solution.py:185
  28.9 7.3 %collective-permute-start.10 = (bf16[136,256]{1,0:T(8,128)(2,1)S(1)}, bf16[136,256]{1,0:T(8,128)(2,1)S(1)}, u32[]{:S(2)}, u32[]{:S(2)}) collective-permute-start(bf16[136,256]{1,0:T(8,128)(2,1)S(1)} %get-tuple-element.19), channel_id=1, source_target_pairs={{0,8},{1,9},{2,10},{3,11},{4,12},{5,13},{6,14},{7,15},{8,16},{9,17... | collective-permute-start | bytes 208904 | tf_op jit(solution)/shard_map/ppermute | solution.py:185
  32.1 5.2 %collective-permute-start.6 = (bf16[136,256]{1,0:T(8,128)(2,1)S(1)}, bf16[136,256]{1,0:T(8,128)(2,1)S(1)}, u32[]{:S(2)}, u32[]{:S(2)}) collective-permute-start(bf16[136,256]{1,0:T(8,128)(2,1)S(1)} %get-tuple-element.15), channel_id=1, source_target_pairs={{0,24},{1,25},{2,26},{3,27},{4,28},{5,29},{6,30},{7,31},{8,0},{9,1... | collective-permute-start | bytes 208904 | tf_op jit(solution)/shard_map/ppermute | solution.py:185
